TPU v7x, 32 devices: a whole 2x2x4 slice. The times are simulated.
32 devices in a mesh: layer: 4 (over y, x), latent: 8 (over z, core).
Axes of the slice: x: 2, y: 2, z: 4, core: 2. Of those that a mesh axis runs over, the one named last changes fastest.
Arguments:
- acts: bfloat16 [128, 4, 2304], P('latent', 'layer'), may hold values from -6 to 6
- enc_weight: bfloat16 [4, 2304, 4096], P('layer', None, 'latent'), may hold values from -0.0625 to 0.0625
- enc_bias: float32 [4096], P('latent'), may hold values from -3 to 3
- dec_weight: bfloat16 [4, 4096, 2304], P('layer', 'latent'), may hold values from -0.125 to 0.125
- dec_bias: float32 [4, 2304], P('layer'), may hold values from -4 to 4
Outputs:
- recon: bfloat16 [128, 4, 2304], P('latent', 'layer')
All inputs are finite; a program needn't handle non-finite values.
Results may differ from a plain program's by a relative error of at most 0.023.
Values may be sent and summed in bfloat16 or wider, within the bound.
No kernel may reach another device: no remote copies, remote signals or barrier semaphores. Data moves between devices by JAX's collectives and lax.ppermute only.
A program may use at most 64 MiB of HBM per device.

v0:
```python
import jax
import jax.numpy as jnp
from jax import lax
from jax.sharding import PartitionSpec as P


def on_device(acts, enc_weight, enc_bias, dec_weight, dec_bias):
    lay_count = acts.shape[1]
    width = acts.shape[2]
    panel = enc_weight.shape[2]
    flat_enc = enc_weight.reshape(lay_count * width, panel)
    piece = lax.all_gather(acts, "latent", axis=0, tiled=True)
    flat_rows = piece.reshape(piece.shape[0], lay_count * width)
    local_pre = jnp.dot(flat_rows, flat_enc, preferred_element_type=jnp.float32)
    summed = lax.psum_scatter(
        local_pre.astype(jnp.bfloat16), "layer", scatter_dimension=0, tiled=True
    ).astype(jnp.float32)
    own_codes = jnp.maximum(summed + enc_bias[None, :], 0.0).astype(jnp.bfloat16)
    codes = lax.all_gather(own_codes, "layer", axis=0, tiled=True)
    total = lax.psum_scatter(
        jnp.einsum("tk,lkd->tld", codes, dec_weight, preferred_element_type=jnp.float32).astype(
            jnp.bfloat16
        ),
        "latent",
        scatter_dimension=0,
        tiled=True,
    ).astype(jnp.float32)
    return (total + dec_bias[None, :, :]).astype(jnp.bfloat16)


def solution(mesh):
    return jax.shard_map(
        on_device,
        mesh=mesh,
        in_specs=(
            P("latent", "layer", None),
            P("layer", None, "latent"),
            P("latent"),
            P("layer", "latent", None),
            P("layer", None),
        ),
        out_specs=P("latent", "layer", None),
        check_vma=False,
    )
```

profile of v0, /device:TPU:0, one launch (start us, length us, event | category | flops | bytes accessed | tf_op | source)
XLA Modules:
  0.0 102.5 jit_solution(5473022016814519974)
XLA Ops:
  6.5 0.0 copy-start
  6.5 0.0 copy-start.2
  6.5 0.0 reduce-scatter.3.cloned.1.call-start
  6.5 17.0 %all_gather.6 = bf16[128,1,2304]{2,0,1:T(8,128)(2,1)S(1)} all-gather(bf16[16,1,2304]{2,0,1:T(8,128)(2,1)} %param.5), channel_id=1, replica_groups=mesh['layer'=4,'latent'=8] {'latent'}, dimensions={0}, use_global_device_ids=true | all-gather | bytes 663552 | tf_op jit(solution)/shard_map/all_gather | solution.py:12
  23.5 2.8 %fusion.4 = bf16[128,512]{1,0:T(8,128)(2,1)} fusion(bf16[1,2304,512]{2,1,0:T(8,128)(2,1)} %param.6, bf16[128,1,2304]{2,0,1:T(8,128)(2,1)S(1)} %all_gather.6), kind=kOutput, calls=%fused_computation.5 | convolution fusion | flops 302055424 | bytes 3080192 | tf_op jit(solution)/shard_map/dot_general | solution.py:14
  26.3 0.0 copy-start.1
  26.3 0.0 reduce-scatter.3.cloned.1.call-update
  26.3 0.0 reduce-scatter.5.cloned.1.call-start
  26.4 25.4 %reduce-scatter.3.cloned.1.call-done = bf16[32,512]{1,0:T(8,128)(2,1)} async-done(((bf16[128,512]{1,0:T(8,128)(2,1)}), bf16[32,512]{1,0:T(8,128)(2,1)}) %reduce-scatter.3.cloned.1.call-update) | async-done | bytes 32784 | tf_op jit(solution)/shard_map/reduce_scatter | solution.py:15
  51.8 0.0 copy-done.2
  51.8 0.8 maximum_convert_fusion
  52.6 8.5 %all_gather.7 = bf16[128,512]{1,0:T(8,128)(2,1)S(1)} all-gather(bf16[32,512]{1,0:T(8,128)(2,1)S(1)} %maximum_convert_fusion), channel_id=1, replica_groups=mesh['layer'=4,'latent'=8] {'layer'}, dimensions={0}, use_global_device_ids=true | all-gather | bytes 163840 | tf_op jit(solution)/shard_map/all_gather | solution.py:19
  61.0 0.0 copy-done
  61.0 1.3 %fusion = bf16[128,1,2304]{2,0,1:T(8,128)(2,1)} fusion(bf16[128,512]{1,0:T(8,128)(2,1)S(1)} %all_gather.7, bf16[1,512,2304]{2,1,0:T(8,128)(2,1)S(1)} %copy-done), kind=kOutput, calls=%fused_computation.1 | convolution fusion | flops 302284800 | bytes 3080192 | tf_op jit(solution)/shard_map/tk,lkd->tld/dot_general | solution.py:21
  62.3 0.0 reduce-scatter.5.cloned.1.call-update
  62.4 0.0 copy-done.1
  62.4 31.7 %reduce-scatter.5.cloned.1.call-done = bf16[16,1,2304]{2,0,1:T(8,128)(2,1)} async-done(((bf16[128,1,2304]{2,0,1:T(8,128)(2,1)}), bf16[16,1,2304]{2,0,1:T(8,128)(2,1)}) %reduce-scatter.5.cloned.1.call-update) | async-done | bytes 73744 | tf_op jit(solution)/shard_map/reduce_scatter | solution.py:20
  94.1 1.5 %add_convert_fusion = bf16[16,1,2304]{2,0,1:T(8,128)(2,1)} fusion(bf16[16,1,2304]{2,0,1:T(8,128)(2,1)} %reduce-scatter.5.cloned.1.call-done, f32[2304]{0:T(1024)S(1)} %reduce), kind=kLoop, calls=%fused_computation.7 | loop fusion | flops 110592 | bytes 156672 | tf_op jit(solution)/shard_map/convert_element_type | solution.py:28
  (1 shorter events, 0.0 us)
Async XLA Ops:
  6.5 54.5 %copy-start = (bf16[1,512,2304]{2,1,0:T(8,128)(2,1)S(1)}, bf16[1,512,2304]{2,1,0:T(8,128)(2,1)}, u32[]{:S(2)}) copy-start(bf16[1,512,2304]{2,1,0:T(8,128)(2,1)} %param.8) | copy-start | bytes 7077892
  6.5 45.2 %copy-start.2 = (f32[512]{0:T(512)S(1)}, f32[512]{0:T(512)}, u32[]{:S(2)}) copy-start(f32[512]{0:T(512)} %param.7) | copy-start | bytes 6148
  6.5 45.2 %reduce-scatter.3.cloned.1.call-start = ((), (), s32[]{:S(2)}) async-start(), calls=%async_computation.2 | async-start | bytes 163840 | tf_op jit(solution)/shard_map/reduce_scatter | solution.py:15
  26.3 36.1 %copy-start.1 = (f32[1,2304]{1,0:T(1,128)S(1)}, f32[1,2304]{1,0:T(1,128)}, u32[]{:S(2)}) copy-start(f32[1,2304]{1,0:T(1,128)} %param.9) | copy-start | bytes 27652
  26.3 67.8 %reduce-scatter.5.cloned.1.call-start = ((), (), s32[]{:S(2)}) async-start(), calls=%async_computation.3 | async-start | bytes 663552 | tf_op jit(solution)/shard_map/reduce_scatter | solution.py:20
Sparse Core Ops, SparseCore 0:
  26.4 25.2 reduce-scatter.2
  62.5 31.6 reduce-scatter.4
where the time goes:
time: 103 us
  waiting for transfers between devices  57.2 us (56%)
  blocking collectives  25.4 us (25%)
  between operations  13.4 us (13%)
  matrix products  4.1 us (4%)
  other arithmetic  2.33 us (2%)
    reduce_scatter x1, waiting for transfers between devices, on_device(): lax.psum_scatter(jnp.einsum('tk,lkd->tld', codes, dec_weight, preferred_e...  31.7 us
    reduce_scatter x1, waiting for transfers between devices, on_device(): lax.psum_scatter(local_pre.astype(jnp.bfloat16), 'layer', scatter_dimensi...  25.4 us
    all_gather x1, blocking collectives, on_device(): piece = lax.all_gather(acts, 'latent', axis=0, tiled=True)  17 us
    all_gather x1, blocking collectives, on_device(): codes = lax.all_gather(own_codes, 'layer', axis=0, tiled=True)  8.48 us
    dot_general x1, matrix products, on_device(): local_pre = jnp.dot(flat_rows, flat_enc, preferred_element_type=jnp.float32)  2.79 us
  transfers between devices with their start and end apart: 2, of which 2 were waited for; matrix products, arithmetic and copies ran while one was open for 0% of the time, Pallas kernels for 0%

commit v1 on v0

v1 whole, which is shorter than its diff:
```python
import jax
import jax.numpy as jnp
from jax import lax
from jax.sharding import PartitionSpec as P


def partners(count):
    pairs = count // 2
    if pairs & (pairs - 1):
        return [[(i, (i + 2 * k) % count) for i in range(count)] for k in range(1, pairs)]
    return [[(i, i ^ (2 * k)) for i in range(count)] for k in range(1, pairs)]


def make(mesh):
    latent = mesh.shape["latent"]
    swap = [(i, i ^ 1) for i in range(latent)]
    rounds = partners(latent)
    back = [[(j, i) for i, j in table] for table in rounds]

    def on_device(acts, enc_weight, enc_bias, dec_weight, dec_bias):
        own = acts[:, 0, :]
        rows = own.shape[0]
        shards = [own] + [lax.ppermute(own, "latent", table) for table in rounds]
        near = jnp.concatenate(shards, axis=0)
        far = lax.ppermute(near, "latent", swap)
        tokens = jnp.concatenate([near, far], axis=0)
        pre = jnp.dot(tokens, enc_weight[0], preferred_element_type=jnp.float32)
        shares = lax.all_gather(pre.astype(jnp.bfloat16), "layer", axis=0, tiled=False)
        total = jnp.sum(shares.astype(jnp.float32), axis=0) + enc_bias[None, :]
        codes = jnp.maximum(total, 0.0).astype(jnp.bfloat16)
        half = near.shape[0]
        out = jnp.dot(codes, dec_weight[0], preferred_element_type=jnp.float32).astype(jnp.bfloat16)
        got = lax.ppermute(out[half:], "latent", swap)
        mine = (out[:half].astype(jnp.float32) + got.astype(jnp.float32)).astype(jnp.bfloat16)
        acc = mine[:rows].astype(jnp.float32)
        for k, table in enumerate(back):
            acc = acc + lax.ppermute(mine[(k + 1) * rows : (k + 2) * rows], "latent", table).astype(jnp.float32)
        return (acc + dec_bias).astype(jnp.bfloat16)[:, None, :]

    return on_device


def solution(mesh):
    return jax.shard_map(
        make(mesh),
        mesh=mesh,
        in_specs=(
            P("latent", "layer", None),
            P("layer", None, "latent"),
            P("latent"),
            P("layer", "latent", None),
            P("layer", None),
        ),
        out_specs=P("latent", "layer", None),
        check_vma=False,
    )
```

time: 103 us -> 39.9 us (0.39)
  waiting for transfers between devices: 57.2 us -> 13.8 us
  blocking collectives: 25.4 us -> 10 us
  between operations: 13.4 us -> 0.13 us
  starting transfers between devices: 0.04 us -> 10.2 us
  matrix products: 4.1 us -> 2.63 us
  local copies, waits for them, and re-layouts: 0.01 us -> 1.05 us
    reduce_scatter x2 -> x0, waiting for transfers between devices: 57.1 us -> none  [the longest x1 31.7 us: on_device(): lax.psum_scatter(jnp.einsum('tk,lkd->tld', codes, dec_weight, preferred_e...]
    all_gather x2 -> x1, blocking collectives: 25.4 us -> 10 us  [on_device(): lax.all_gather(pre.astype(jnp.bfloat16), 'layer', axis=0, tiled=False)]
    ppermute x0 -> x8, waiting for transfers between devices: none -> 13.8 us  [the longest x3 5.5 us: on_device(): shards = [own] + [lax.ppermute(own, 'latent', table) for table in rounds]]
    ppermute x0 -> x8, starting transfers between devices: none -> 10.2 us  [the longest x3 5.64 us: on_device(): shards = [own] + [lax.ppermute(own, 'latent', table) for table in rounds]]
    convert_element_type x2 -> x1, other arithmetic: 2.3 us -> 0.08 us  [on_device(): (out[:half].astype(jnp.float32) + got.astype(jnp.float32)).astype(jnp.bfl...]
    dot_general x2, matrix products: 4.1 us -> 2.63 us  [the longest x1 2.15 us: on_device(): pre = jnp.dot(tokens, enc_weight[0], preferred_element_type=jnp.float32)]
  transfers between devices with their start and end apart: 2 -> 8, of which waited for: 2 -> 6; matrix products, arithmetic and copies ran while one was open for 0% -> 3% of each run, Pallas kernels for 0% -> 0%
where the time goes in v1:
time: 39.9 us; the launch traced here: 39.7 us
  waiting for transfers between devices  13.8 us (35%)
  starting transfers between devices  10.2 us (26%)
  blocking collectives  10 us (25%)
  matrix products  2.63 us (7%)
  other arithmetic  1.76 us (4%)
  local copies, waits for them, and re-layouts  1.05 us (3%)
    all_gather x1, blocking collectives, on_device(): lax.all_gather(pre.astype(jnp.bfloat16), 'layer', axis=0, tiled=False)  10 us
    ppermute x3, starting transfers between devices, on_device(): shards = [own] + [lax.ppermute(own, 'latent', table) for table in rounds]  5.64 us
    ppermute x3, waiting for transfers between devices, on_device(): shards = [own] + [lax.ppermute(own, 'latent', table) for table in rounds]  5.5 us
    ppermute x3, waiting for transfers between devices, on_device(): lax.ppermute(mine[(k + 1) * rows:(k + 2) * rows], 'latent', table)  5.21 us
    ppermute x3, starting transfers between devices, on_device(): lax.ppermute(mine[(k + 1) * rows:(k + 2) * rows], 'latent', table)  4.45 us
    dot_general x1, matrix products, on_device(): pre = jnp.dot(tokens, enc_weight[0], preferred_element_type=jnp.float32)  2.15 us
    ppermute x1, waiting for transfers between devices, on_device(): got = lax.ppermute(out[half:], 'latent', swap)  1.57 us
    ppermute x1, waiting for transfers between devices, on_device(): far = lax.ppermute(near, 'latent', swap)  1.52 us
  transfers between devices with their start and end apart: 8, of which 6 were waited for; matrix products, arithmetic and copies ran while one was open for 3% of the time, Pallas kernels for 0%

profile of v1, /device:TPU:0, one launch (start us, length us, event | category | flops | bytes accessed | tf_op | source)
XLA Modules:
  0.0 39.7 jit_solution(5615761467282382837)
XLA Ops:
  0.0 0.0 copy-start
  0.0 3.1 %collective-permute-start = (bf16[16,2304]{1,0:T(8,128)(2,1)}, bf16[16,2304]{1,0:T(8,128)(2,1)S(1)}, u32[]{:S(2)}, u32[]{:S(2)}) collective-permute-start(bf16[16,2304]{1,0:T(8,128)(2,1)} %bitcast.16), channel_id=1, source_target_pairs={{0,2},{1,3},{2,0},{3,1},{4,6},{5,7},{6,4},{7,5},{8,10},{9,11},{10,... | collective-permute-start | bytes 221192 | tf_op jit(solution)/shard_map/ppermute | solution.py:23
  3.1 2.6 %collective-permute-start.1 = (bf16[16,2304]{1,0:T(8,128)(2,1)}, bf16[16,2304]{1,0:T(8,128)(2,1)S(1)}, u32[]{:S(2)}, u32[]{:S(2)}) collective-permute-start(bf16[16,2304]{1,0:T(8,128)(2,1)} %bitcast.17), channel_id=1, source_target_pairs={{0,4},{1,5},{2,6},{3,7},{4,0},{5,1},{6,2},{7,3},{8,12},{9,13},{10,... | collective-permute-start | bytes 221192 | tf_op jit(solution)/shard_map/ppermute | solution.py:23
  5.6 0.0 collective-permute-start.2
  5.6 1.0 %constant_dynamic-update-slice_fusion.4 = bf16[128,2304]{1,0:T(8,128)(2,1)S(1)} fusion(bf16[16,1,2304]{2,0,1:T(8,128)(2,1)} %param.5), kind=kLoop, calls=%fused_computation.17 | loop fusion | bytes 147456
  6.6 0.0 collective-permute-done
  6.6 4.5 %collective-permute-done.1 = bf16[16,2304]{1,0:T(8,128)(2,1)S(1)} collective-permute-done((bf16[16,2304]{1,0:T(8,128)(2,1)}, bf16[16,2304]{1,0:T(8,128)(2,1)S(1)}, u32[]{:S(2)}, u32[]{:S(2)}) %collective-permute-start.1) | collective-permute-done | bytes 73760 | tf_op jit(solution)/shard_map/ppermute | solution.py:23
  11.1 1.0 %collective-permute-done.2 = bf16[16,2304]{1,0:T(8,128)(2,1)S(1)} collective-permute-done((bf16[16,2304]{1,0:T(8,128)(2,1)}, bf16[16,2304]{1,0:T(8,128)(2,1)S(1)}, u32[]{:S(2)}, u32[]{:S(2)}) %collective-permute-start.2) | collective-permute-done | bytes 73760 | tf_op jit(solution)/shard_map/ppermute | solution.py:23
  12.1 0.9 %pad_maximum_fusion = bf16[64,2304]{1,0:T(8,128)(2,1)S(1)} fusion(bf16[16,2304]{1,0:T(8,128)(2,1)S(1)} %collective-permute-done.2, bf16[16,2304]{1,0:T(8,128)(2,1)S(1)} %collective-permute-done.1, bf16[16,2304]{1,0:T(8,128)(2,1)S(1)} %collective-permute-done, bf16[16,2304]{1,0:T(8,128)(2,1)} %bitcast.19), kind=kLoop, calls=%fused_computation.7 | loop fusion | flops 1179648 | bytes 589824 | tf_op jit(solution)/shard_map/concatenate | solution.py:24
  13.0 0.1 collective-permute-start.3
  13.1 1.5 %collective-permute-done.3 = bf16[64,2304]{1,0:T(8,128)(2,1)S(1)} collective-permute-done((bf16[64,2304]{1,0:T(8,128)(2,1)S(1)}, bf16[64,2304]{1,0:T(8,128)(2,1)S(1)}, u32[]{:S(2)}, u32[]{:S(2)}) %collective-permute-start.3) | collective-permute-done | bytes 294944 | tf_op jit(solution)/shard_map/ppermute | solution.py:25
  14.7 0.0 copy-start.2
  14.7 2.1 %fusion.3 = bf16[128,512]{1,0:T(8,128)(2,1)S(1)} fusion(bf16[128,2304]{1,0:T(8,128)(2,1)S(1)} %constant_dynamic-update-slice_fusion, bf16[1,2304,512]{2,1,0:T(8,128)(2,1)} %param.6), kind=kOutput, calls=%fused_computation.4 | convolution fusion | flops 302055424 | bytes 3080192 | tf_op jit(solution)/shard_map/dot_general | solution.py:27
  16.9 10.0 %all-gather = bf16[512,512]{1,0:T(8,128)(2,1)S(1)} all-gather(bf16[128,512]{1,0:T(8,128)(2,1)S(1)} %fusion.3), channel_id=2, replica_groups=mesh['layer'=4,'latent'=8] {'layer'}, dimensions={0}, use_global_device_ids=true | all-gather | bytes 655360 | tf_op jit(solution)/shard_map/all_gather | solution.py:28
  26.9 0.1 convert_reduce_fusion
  27.0 0.0 copy-done
  27.0 0.0 copy-done.2
  27.0 0.0 copy-start.1
  27.0 0.5 %convolution_convert_fusion = bf16[128,2304]{1,0:T(8,128)(2,1)S(1)} fusion(bf16[1,512,2304]{2,1,0:T(8,128)(2,1)S(1)} %copy-done, f32[128,512]{1,0:T(8,128)S(1)} %convert_reduce_fusion, f32[512]{0:T(512)S(1)} %copy-done.2), kind=kOutput, calls=%fused_computation | convolution fusion | flops 302481408 | bytes 3213312 | tf_op jit(solution)/shard_map/dot_general | solution.py:32
  27.5 0.1 collective-permute-start.4
  27.6 1.6 %collective-permute-done.4 = bf16[64,2304]{1,0:T(8,128)(2,1)S(1)} collective-permute-done((bf16[64,2304]{1,0:T(8,128)(2,1)S(1)}, bf16[64,2304]{1,0:T(8,128)(2,1)S(1)}, u32[]{:S(2)}, u32[]{:S(2)}) %collective-permute-start.4) | collective-permute-done | bytes 294944 | tf_op jit(solution)/shard_map/ppermute | solution.py:33
  29.2 0.1 add_convert_fusion
  29.3 2.3 %collective-permute-start.7 = (bf16[16,2304]{1,0:T(8,128)(2,1)S(1)}, bf16[16,2304]{1,0:T(8,128)(2,1)S(1)}, u32[]{:S(2)}, u32[]{:S(2)}) collective-permute-start(bf16[16,2304]{1,0:T(8,128)(2,1)S(1)} %get-tuple-element.6), channel_id=1, source_target_pairs={{6,0},{7,1},{4,2},{5,3},{2,4},{3,5},{0,6},{1,7},{14,8},{15,9},{12,... | collective-permute-start | bytes 221192 | tf_op jit(solution)/shard_map/ppermute | solution.py:37
  31.6 0.3 collective-permute-start.6
  31.9 1.8 %collective-permute-start.5 = (bf16[16,2304]{1,0:T(8,128)(2,1)S(1)}, bf16[16,2304]{1,0:T(8,128)(2,1)S(1)}, u32[]{:S(2)}, u32[]{:S(2)}) collective-permute-start(bf16[16,2304]{1,0:T(8,128)(2,1)S(1)} %get-tuple-element.5), channel_id=1, source_target_pairs={{2,0},{3,1},{0,2},{1,3},{6,4},{7,5},{4,6},{5,7},{10,8},{11,9},{8,1... | collective-permute-start | bytes 221192 | tf_op jit(solution)/shard_map/ppermute | solution.py:37
  33.7 0.0 copy-done.1
  33.8 2.5 %collective-permute-done.7 = bf16[16,2304]{1,0:T(8,128)(2,1)S(1)} collective-permute-done((bf16[16,2304]{1,0:T(8,128)(2,1)S(1)}, bf16[16,2304]{1,0:T(8,128)(2,1)S(1)}, u32[]{:S(2)}, u32[]{:S(2)}) %collective-permute-start.7) | collective-permute-done | bytes 73760 | tf_op jit(solution)/shard_map/ppermute | solution.py:37
  36.3 2.7 %collective-permute-done.6 = bf16[16,2304]{1,0:T(8,128)(2,1)S(1)} collective-permute-done((bf16[16,2304]{1,0:T(8,128)(2,1)S(1)}, bf16[16,2304]{1,0:T(8,128)(2,1)S(1)}, u32[]{:S(2)}, u32[]{:S(2)}) %collective-permute-start.6) | collective-permute-done | bytes 73760 | tf_op jit(solution)/shard_map/ppermute | solution.py:37
  39.0 0.0 collective-permute-done.5
  39.0 0.7 %fusion.8 = bf16[16,1,2304]{2,0,1:T(8,128)(2,1)} fusion(bf16[16,2304]{1,0:T(8,128)(2,1)S(1)} %collective-permute-done.7, bf16[16,2304]{1,0:T(8,128)(2,1)S(1)} %collective-permute-done.6, bf16[16,2304]{1,0:T(8,128)(2,1)S(1)} %collective-permute-done.5, bf16[64,2304]{1,0:T(8,128)(2,1)S(1)} %add_convert_fusion, f32[2304]{0:T(1024)S(1)} %reduce), kind=kLoop, calls=%fused_computation.12 | loop fusion | flops 331776 | bytes 377856 | tf_op jit(solution)/shard_map/broadcast_in_dim | solution.py:38
  (7 shorter events, 0.1 us)
Async XLA Ops:
  0.0 27.0 %copy-start = (bf16[1,512,2304]{2,1,0:T(8,128)(2,1)S(1)}, bf16[1,512,2304]{2,1,0:T(8,128)(2,1)}, u32[]{:S(2)}) copy-start(bf16[1,512,2304]{2,1,0:T(8,128)(2,1)} %param.8) | copy-start | bytes 7077892
  0.0 6.6 %collective-permute-start = (bf16[16,2304]{1,0:T(8,128)(2,1)}, bf16[16,2304]{1,0:T(8,128)(2,1)S(1)}, u32[]{:S(2)}, u32[]{:S(2)}) collective-permute-start(bf16[16,2304]{1,0:T(8,128)(2,1)} %bitcast.16), channel_id=1, source_target_pairs={{0,2},{1,3},{2,0},{3,1},{4,6},{5,7},{6,4},{7,5},{8,10},{9,11},{10,... | collective-permute-start | bytes 221192 | tf_op jit(solution)/shard_map/ppermute | solution.py:23
  3.1 8.0 %collective-permute-start.1 = (bf16[16,2304]{1,0:T(8,128)(2,1)}, bf16[16,2304]{1,0:T(8,128)(2,1)S(1)}, u32[]{:S(2)}, u32[]{:S(2)}) collective-permute-start(bf16[16,2304]{1,0:T(8,128)(2,1)} %bitcast.17), channel_id=1, source_target_pairs={{0,4},{1,5},{2,6},{3,7},{4,0},{5,1},{6,2},{7,3},{8,12},{9,13},{10,... | collective-permute-start | bytes 221192 | tf_op jit(solution)/shard_map/ppermute | solution.py:23
  5.6 6.5 %collective-permute-start.2 = (bf16[16,2304]{1,0:T(8,128)(2,1)}, bf16[16,2304]{1,0:T(8,128)(2,1)S(1)}, u32[]{:S(2)}, u32[]{:S(2)}) collective-permute-start(bf16[16,2304]{1,0:T(8,128)(2,1)} %bitcast.18), channel_id=1, source_target_pairs={{0,6},{1,7},{2,4},{3,5},{4,2},{5,3},{6,0},{7,1},{8,14},{9,15},{10,... | collective-permute-start | bytes 221192 | tf_op jit(solution)/shard_map/ppermute | solution.py:23
  13.0 1.6 %collective-permute-start.3 = (bf16[64,2304]{1,0:T(8,128)(2,1)S(1)}, bf16[64,2304]{1,0:T(8,128)(2,1)S(1)}, u32[]{:S(2)}, u32[]{:S(2)}) collective-permute-start(bf16[64,2304]{1,0:T(8,128)(2,1)S(1)} %pad_maximum_fusion), channel_id=1, source_target_pairs={{0,1},{1,0},{2,3},{3,2},{4,5},{5,4},{6,7},{7,6},{8,9},{9,8},{10,11... | collective-permute-start | bytes 884744 | tf_op jit(solution)/shard_map/ppermute | solution.py:25
  14.7 12.3 %copy-start.2 = (f32[512]{0:T(512)S(1)}, f32[512]{0:T(512)}, u32[]{:S(2)}) copy-start(f32[512]{0:T(512)} %param.7) | copy-start | bytes 6148
  27.0 6.7 %copy-start.1 = (f32[1,2304]{1,0:T(1,128)S(1)}, f32[1,2304]{1,0:T(1,128)}, u32[]{:S(2)}) copy-start(f32[1,2304]{1,0:T(1,128)} %param.9) | copy-start | bytes 27652
  27.5 1.6 %collective-permute-start.4 = (bf16[64,2304]{1,0:T(8,128)(2,1)S(1)}, bf16[64,2304]{1,0:T(8,128)(2,1)S(1)}, u32[]{:S(2)}, u32[]{:S(2)}) collective-permute-start(bf16[64,2304]{1,0:T(8,128)(2,1)S(1)} %slice.25), channel_id=1, source_target_pairs={{0,1},{1,0},{2,3},{3,2},{4,5},{5,4},{6,7},{7,6},{8,9},{9,8},{10,11... | collective-permute-start | bytes 884744 | tf_op jit(solution)/shard_map/ppermute | solution.py:33
  29.3 7.0 %collective-permute-start.7 = (bf16[16,2304]{1,0:T(8,128)(2,1)S(1)}, bf16[16,2304]{1,0:T(8,128)(2,1)S(1)}, u32[]{:S(2)}, u32[]{:S(2)}) collective-permute-start(bf16[16,2304]{1,0:T(8,128)(2,1)S(1)} %get-tuple-element.6), channel_id=1, source_target_pairs={{6,0},{7,1},{4,2},{5,3},{2,4},{3,5},{0,6},{1,7},{14,8},{15,9},{12,... | collective-permute-start | bytes 221192 | tf_op jit(solution)/shard_map/ppermute | solution.py:37
  31.6 7.4 %collective-permute-start.6 = (bf16[16,2304]{1,0:T(8,128)(2,1)S(1)}, bf16[16,2304]{1,0:T(8,128)(2,1)S(1)}, u32[]{:S(2)}, u32[]{:S(2)}) collective-permute-start(bf16[16,2304]{1,0:T(8,128)(2,1)S(1)} %get-tuple-element.7), channel_id=1, source_target_pairs={{4,0},{5,1},{6,2},{7,3},{0,4},{1,5},{2,6},{3,7},{12,8},{13,9},{14,... | collective-permute-start | bytes 221192 | tf_op jit(solution)/shard_map/ppermute | solution.py:37
  31.9 7.1 %collective-permute-start.5 = (bf16[16,2304]{1,0:T(8,128)(2,1)S(1)}, bf16[16,2304]{1,0:T(8,128)(2,1)S(1)}, u32[]{:S(2)}, u32[]{:S(2)}) collective-permute-start(bf16[16,2304]{1,0:T(8,128)(2,1)S(1)} %get-tuple-element.5), channel_id=1, source_target_pairs={{2,0},{3,1},{0,2},{1,3},{6,4},{7,5},{4,6},{5,7},{10,8},{11,9},{8,1... | collective-permute-start | bytes 221192 | tf_op jit(solution)/shard_map/ppermute | solution.py:37

commit v2 on v1

v2 whole, which is shorter than its diff:
```python
import jax
import jax.numpy as jnp
from jax import lax
from jax.experimental import pallas as pl
from jax.experimental.pallas import tpu as pltpu
from jax.sharding import PartitionSpec as P


def meetings(count):
    chips = count // 2
    assert chips & (chips - 1) == 0
    return [[(i, i ^ (2 * k + 1)) for i in range(count)] for k in range(chips - 1, 0, -1)]


def doublings(count):
    assert count & (count - 1) == 0
    return [[(i, i ^ (1 << k)) for i in range(count)] for k in range(count.bit_length() - 1)]


def reverse(table):
    return [(j, i) for i, j in table]


def staged(x):
    def body(src, dst, sem):
        copy = pltpu.make_async_copy(src, dst, sem)
        copy.start()
        copy.wait()

    return pl.pallas_call(
        body,
        out_shape=pltpu.VMEM(x.shape, x.dtype),
        in_specs=[pl.BlockSpec(memory_space=pl.ANY)],
        out_specs=pl.BlockSpec(memory_space=pltpu.VMEM),
        scratch_shapes=[pltpu.SemaphoreType.DMA],
        compiler_params=pltpu.CompilerParams(vmem_limit_bytes=4 << 20),
    )(x)


def make(mesh):
    latent, layer = mesh.shape["latent"], mesh.shape["layer"]
    swap = [(i, i ^ 1) for i in range(latent)]
    rounds = meetings(latent)
    steps = doublings(layer)
    cut = len(rounds) // 2

    def on_device(acts, enc_weight, enc_bias, dec_weight, dec_bias):
        own = acts[:, 0, :]
        rows = own.shape[0]

        def encode(shards):
            tokens = jnp.concatenate(shards, axis=0)
            pre = jnp.concatenate(
                [
                    jnp.dot(tokens, enc_near, preferred_element_type=jnp.float32),
                    jnp.dot(tokens, enc_far, preferred_element_type=jnp.float32),
                ],
                axis=0,
            )
            return pre

        def mix(steps, pre):
            for table in steps:
                got = lax.ppermute(pre.astype(jnp.bfloat16), "layer", table)
                pre = pre + got.astype(jnp.float32)
            return pre

        def decode(total):
            half = total.shape[0] // 2
            code = jnp.maximum(total[:half] + enc_bias[None, :], 0.0).astype(jnp.bfloat16)
            code_far = jnp.maximum(total[half:] + bias_far[None, :], 0.0).astype(jnp.bfloat16)
            return jnp.dot(code, dec, preferred_element_type=jnp.float32) + jnp.dot(
                code_far, dec_far, preferred_element_type=jnp.float32
            )

        got = [lax.ppermute(own, "latent", table) for table in rounds]
        enc = enc_weight[0]
        dec = dec_weight[0]
        enc_far = lax.ppermute(enc, "latent", swap)
        dec_far = lax.ppermute(dec, "latent", swap)
        bias_far = lax.ppermute(enc_bias, "latent", swap)
        enc_near = staged(enc)
        first = mix(steps, encode([own] + got[:cut]))
        second = mix(steps[::-1], encode(got[cut:]))
        out = decode(first)
        acc = out[:rows] + dec_bias
        out = out.astype(jnp.bfloat16)
        back = [
            lax.ppermute(out[(k + 1) * rows : (k + 2) * rows], "latent", reverse(table))
            for k, table in enumerate(rounds[:cut])
        ]
        out = decode(second).astype(jnp.bfloat16)
        back += [
            lax.ppermute(out[k * rows : (k + 1) * rows], "latent", reverse(table))
            for k, table in enumerate(rounds[cut:])
        ]
        for part in back:
            acc = acc + part.astype(jnp.float32)
        return acc.astype(jnp.bfloat16)[:, None, :]

    return on_device


def solution(mesh):
    return jax.shard_map(
        make(mesh),
        mesh=mesh,
        in_specs=(
            P("latent", "layer", None),
            P("layer", None, "latent"),
            P("latent"),
            P("layer", "latent", None),
            P("layer", None),
        ),
        out_specs=P("latent", "layer", None),
        check_vma=False,
    )
```

time: 39.9 us -> 36.4 us (0.912)
  blocking collectives: 10 us -> 0 us
  starting transfers between devices: 10.2 us -> 15.8 us
  local copies, waits for them, and re-layouts: 1.05 us -> 2.59 us
  matrix products: 2.63 us -> 3.96 us
  waiting for transfers between devices: 13.8 us -> 12.7 us
  other arithmetic: 1.76 us -> 0.82 us
    all_gather x1 -> x0, blocking collectives: 10 us -> none  [on_device(): lax.all_gather(pre.astype(jnp.bfloat16), 'layer', axis=0, tiled=False)]
    ppermute x8 -> x13, starting transfers between devices: 10.2 us -> 15.8 us  [the longest x4 6 us: mix(): got = lax.ppermute(pre.astype(jnp.bfloat16), 'layer', table)]
    unnamed x10 -> x11, local copies, waits for them, and re-layouts: 0.99 us -> 2.56 us
    dot_general x2 -> x8, matrix products: 2.63 us -> 3.96 us  [the longest x2 1 us: encode(): jnp.dot(tokens, enc_far, preferred_element_type=jnp.float32)]
    ppermute x8 -> x13, waiting for transfers between devices: 13.8 us -> 12.7 us  [the longest x4 4.21 us: mix(): got = lax.ppermute(pre.astype(jnp.bfloat16), 'layer', table)]
    concatenate x1 -> x0, other arithmetic: 0.9 us -> none  [on_device(): near = jnp.concatenate(shards, axis=0)]
  transfers between devices with their start and end apart: 8 -> 13, of which waited for: 6 -> 8; matrix products, arithmetic and copies ran while one was open for 3% -> 9% of each run, Pallas kernels for 0% -> 0%
where the time goes in v2:
time: 36.4 us; the launch traced here: 36.2 us
  starting transfers between devices  15.8 us (43%)
  waiting for transfers between devices  12.7 us (35%)
  matrix products  3.96 us (11%)
  local copies, waits for them, and re-layouts  2.59 us (7%)
  other arithmetic  0.82 us (2%)
    ppermute x4, starting transfers between devices, mix(): got = lax.ppermute(pre.astype(jnp.bfloat16), 'layer', table)  6 us
    ppermute x3, starting transfers between devices, on_device(): got = [lax.ppermute(own, 'latent', table) for table in rounds]  4.87 us
    ppermute x4, waiting for transfers between devices, mix(): got = lax.ppermute(pre.astype(jnp.bfloat16), 'layer', table)  4.21 us
    ppermute x2, waiting for transfers between devices, on_device(): lax.ppermute(out[k * rows:(k + 1) * rows], 'latent', reverse(table))  3.99 us
    ppermute x2, starting transfers between devices, on_device(): lax.ppermute(out[k * rows:(k + 1) * rows], 'latent', reverse(table))  3.9 us
    unnamed x11, local copies, waits for them, and re-layouts  2.56 us
    ppermute x1, waiting for transfers between devices, on_device(): lax.ppermute(out[(k + 1) * rows:(k + 2) * rows], 'latent', reverse(table))  2.38 us
    ppermute x3, waiting for transfers between devices, on_device(): got = [lax.ppermute(own, 'latent', table) for table in rounds]  2.13 us
  transfers between devices with their start and end apart: 13, of which 8 were waited for; matrix products, arithmetic and copies ran while one was open for 9% of the time, Pallas kernels for 0%

profile of v2, /device:TPU:0, one launch (start us, length us, event | category | flops | bytes accessed | tf_op | source)
XLA Modules:
  0.0 36.2 jit_solution(4894686528366498825)
XLA Ops:
  0.0 0.5 %collective-permute-start.1 = (bf16[2304,512]{1,0:T(8,128)(2,1)}, bf16[2304,512]{1,0:T(8,128)(2,1)S(1)}, u32[]{:S(2)}, u32[]{:S(2)}) collective-permute-start(bf16[2304,512]{1,0:T(8,128)(2,1)} %bitcast.17), channel_id=1, source_target_pairs={{0,1},{1,0},{2,3},{3,2},{4,5},{5,4},{6,7},{7,6},{8,9},{9,8},{10,11... | collective-permute-start | bytes 7077896 | tf_op jit(solution)/shard_map/ppermute | solution.py:79
  0.5 3.7 %collective-permute-start.7 = (bf16[16,2304]{1,0:T(8,128)(2,1)}, bf16[16,2304]{1,0:T(8,128)(2,1)S(1)}, u32[]{:S(2)}, u32[]{:S(2)}) collective-permute-start(bf16[16,2304]{1,0:T(8,128)(2,1)} %bitcast.20), channel_id=1, source_target_pairs={{0,5},{1,4},{2,7},{3,6},{4,1},{5,0},{6,3},{7,2},{8,13},{9,12},{10,... | collective-permute-start | bytes 221192 | tf_op jit(solution)/shard_map/ppermute | solution.py:76
  4.2 1.2 %collective-permute-start.8 = (bf16[16,2304]{1,0:T(8,128)(2,1)}, bf16[16,2304]{1,0:T(8,128)(2,1)S(1)}, u32[]{:S(2)}, u32[]{:S(2)}) collective-permute-start(bf16[16,2304]{1,0:T(8,128)(2,1)} %bitcast.21), channel_id=1, source_target_pairs={{0,3},{1,2},{2,1},{3,0},{4,7},{5,6},{6,5},{7,4},{8,11},{9,10},{10,... | collective-permute-start | bytes 221192 | tf_op jit(solution)/shard_map/ppermute | solution.py:76
  5.4 0.0 collective-permute-start
  5.4 0.5 %collective-permute-start.4 = (f32[512]{0:T(512)}, f32[512]{0:T(512)S(1)}, u32[]{:S(2)}, u32[]{:S(2)}) collective-permute-start(f32[512]{0:T(512)} %param.7), channel_id=1, source_target_pairs={{0,1},{1,0},{2,3},{3,2},{4,5},{5,4},{6,7},{7,6},{8,9},{9,8},{10,11... | collective-permute-start | bytes 6152 | tf_op jit(solution)/shard_map/ppermute | solution.py:81
  5.9 0.0 copy-start
  5.9 1.7 %copy-done = bf16[1,2304,512]{2,1,0:T(8,128)(2,1)S(1)} copy-done((bf16[1,2304,512]{2,1,0:T(8,128)(2,1)S(1)}, bf16[1,2304,512]{2,1,0:T(8,128)(2,1)}, u32[]{:S(2)}) %copy-start) | copy-done | bytes 2359320
  7.5 0.0 copy-start.1
  7.5 0.2 shard_map.55
  7.7 0.0 copy-start.2
  7.7 0.6 %collective-permute-done.7 = bf16[16,2304]{1,0:T(8,128)(2,1)S(1)} collective-permute-done((bf16[16,2304]{1,0:T(8,128)(2,1)}, bf16[16,2304]{1,0:T(8,128)(2,1)S(1)}, u32[]{:S(2)}, u32[]{:S(2)}) %collective-permute-start.7) | collective-permute-done | bytes 73760 | tf_op jit(solution)/shard_map/ppermute | solution.py:76
  8.3 0.9 %copy-done.1 = bf16[1,512,2304]{2,1,0:T(8,128)(2,1)S(1)} copy-done((bf16[1,512,2304]{2,1,0:T(8,128)(2,1)S(1)}, bf16[1,512,2304]{2,1,0:T(8,128)(2,1)}, u32[]{:S(2)}) %copy-start.1) | copy-done | bytes 2359320
  9.2 0.0 collective-permute-start.5
  9.2 0.0 collective-permute-done.8
  9.2 0.5 %fusion.43 = f32[32,512]{1,0:T(8,128)S(1)} fusion(bf16[32,2304]{1,0:T(8,128)(2,1)S(1)} %constant_dynamic-update-slice_fusion, bf16[2304,512]{1,0:T(8,128)(2,1)S(1)} %shard_map.55), kind=kOutput, calls=%fused_computation.56 | convolution fusion | flops 75497472 | bytes 2572288 | tf_op jit(solution)/shard_map/dot_general | solution.py:55
  9.7 1.5 %collective-permute-done = bf16[16,2304]{1,0:T(8,128)(2,1)S(1)} collective-permute-done((bf16[16,2304]{1,0:T(8,128)(2,1)}, bf16[16,2304]{1,0:T(8,128)(2,1)S(1)}, u32[]{:S(2)}, u32[]{:S(2)}) %collective-permute-start) | collective-permute-done | bytes 73760 | tf_op jit(solution)/shard_map/ppermute | solution.py:76
  11.3 0.0 copy-done.2
  11.3 0.5 %fusion.8 = f32[32,512]{1,0:T(8,128)S(1)} fusion(bf16[2304,512]{1,0:T(8,128)(2,1)S(1)} %shard_map.55, bf16[16,2304]{1,0:T(8,128)(2,1)S(1)} %collective-permute-done, bf16[16,2304]{1,0:T(8,128)(2,1)S(1)} %bitcast.23), kind=kOutput, calls=%fused_computation.19 | convolution fusion | flops 75792384 | bytes 2572288 | tf_op jit(solution)/shard_map/dot_general | solution.py:55
  11.8 0.0 collective-permute-done.1
  11.8 0.5 %fusion.44 = f32[32,512]{1,0:T(8,128)S(1)} fusion(bf16[32,2304]{1,0:T(8,128)(2,1)S(1)} %constant_dynamic-update-slice_fusion, bf16[2304,512]{1,0:T(8,128)(2,1)S(1)} %collective-permute-done.1), kind=kOutput, calls=%fused_computation.57 | convolution fusion | flops 75497472 | bytes 2572288 | tf_op jit(solution)/shard_map/dot_general | solution.py:56
  12.3 0.0 copy-start.4
  12.3 1.6 %collective-permute-start.9 = (bf16[64,512]{1,0:T(8,128)(2,1)S(1)}, bf16[64,512]{1,0:T(8,128)(2,1)S(1)}, u32[]{:S(2)}, u32[]{:S(2)}) collective-permute-start(bf16[64,512]{1,0:T(8,128)(2,1)S(1)} %fusion.5), channel_id=1, source_target_pairs={{0,16},{8,24},{16,0},{24,8},{1,17},{9,25},{17,1},{25,9},{2,18},{10... | collective-permute-start | bytes 196616 | tf_op jit(solution)/shard_map/ppermute | solution.py:64
  13.9 0.5 %fusion.7 = f32[32,512]{1,0:T(8,128)S(1)} fusion(bf16[2304,512]{1,0:T(8,128)(2,1)S(1)} %collective-permute-done.1, bf16[16,2304]{1,0:T(8,128)(2,1)S(1)} %collective-permute-done, bf16[16,2304]{1,0:T(8,128)(2,1)S(1)} %bitcast.24), kind=kOutput, calls=%fused_computation.18 | convolution fusion | flops 75792384 | bytes 2572288 | tf_op jit(solution)/shard_map/dot_general | solution.py:56
  14.4 1.6 %collective-permute-start.2 = (bf16[64,512]{1,0:T(8,128)(2,1)S(1)}, bf16[64,512]{1,0:T(8,128)(2,1)S(1)}, u32[]{:S(2)}, u32[]{:S(2)}) collective-permute-start(bf16[64,512]{1,0:T(8,128)(2,1)S(1)} %fusion.6), channel_id=1, source_target_pairs={{0,8},{8,0},{16,24},{24,16},{1,9},{9,1},{17,25},{25,17},{2,10},{10... | collective-permute-start | bytes 196616 | tf_op jit(solution)/shard_map/ppermute | solution.py:64
  16.0 0.9 %collective-permute-done.9 = bf16[64,512]{1,0:T(8,128)(2,1)S(1)} collective-permute-done((bf16[64,512]{1,0:T(8,128)(2,1)S(1)}, bf16[64,512]{1,0:T(8,128)(2,1)S(1)}, u32[]{:S(2)}, u32[]{:S(2)}) %collective-permute-start.9) | collective-permute-done | bytes 65568 | tf_op jit(solution)/shard_map/ppermute | solution.py:64
  16.9 1.6 %collective-permute-start.10 = (bf16[64,512]{1,0:T(8,128)(2,1)S(1)}, bf16[64,512]{1,0:T(8,128)(2,1)S(1)}, u32[]{:S(2)}, u32[]{:S(2)}) collective-permute-start(bf16[64,512]{1,0:T(8,128)(2,1)S(1)} %fusion.11), channel_id=1, source_target_pairs={{0,8},{8,0},{16,24},{24,16},{1,9},{9,1},{17,25},{25,17},{2,10},{10... | collective-permute-start | bytes 196616 | tf_op jit(solution)/shard_map/ppermute | solution.py:64
  18.5 0.3 collective-permute-done.2
  18.8 1.3 %collective-permute-start.3 = (bf16[64,512]{1,0:T(8,128)(2,1)S(1)}, bf16[64,512]{1,0:T(8,128)(2,1)S(1)}, u32[]{:S(2)}, u32[]{:S(2)}) collective-permute-start(bf16[64,512]{1,0:T(8,128)(2,1)S(1)} %fusion.10), channel_id=1, source_target_pairs={{0,16},{8,24},{16,0},{24,8},{1,17},{9,25},{17,1},{25,9},{2,18},{10... | collective-permute-start | bytes 196616 | tf_op jit(solution)/shard_map/ppermute | solution.py:64
  20.1 1.2 %collective-permute-done.10 = bf16[64,512]{1,0:T(8,128)(2,1)S(1)} collective-permute-done((bf16[64,512]{1,0:T(8,128)(2,1)S(1)}, bf16[64,512]{1,0:T(8,128)(2,1)S(1)}, u32[]{:S(2)}, u32[]{:S(2)}) %collective-permute-start.10) | collective-permute-done | bytes 65568 | tf_op jit(solution)/shard_map/ppermute | solution.py:64
  21.3 1.8 %collective-permute-done.3 = bf16[64,512]{1,0:T(8,128)(2,1)S(1)} collective-permute-done((bf16[64,512]{1,0:T(8,128)(2,1)S(1)}, bf16[64,512]{1,0:T(8,128)(2,1)S(1)}, u32[]{:S(2)}, u32[]{:S(2)}) %collective-permute-start.3) | collective-permute-done | bytes 65568 | tf_op jit(solution)/shard_map/ppermute | solution.py:64
  23.1 0.0 copy-done.4
  23.1 0.5 %fusion.20 = f32[32,2304]{1,0:T(8,128)S(1)} fusion(f32[64,512]{1,0:T(8,128)S(1)} %convert_add_fusion.2, f32[512]{0:T(512)S(1)} %copy-done.4, bf16[1,512,2304]{2,1,0:T(8,128)(2,1)S(1)} %copy-done.1), kind=kOutput, calls=%fused_computation.35 | convolution fusion | flops 75546624 | bytes 2721792 | tf_op jit(solution)/shard_map/dot_general | solution.py:72
  23.6 0.5 %fusion.23 = f32[32,2304]{1,0:T(8,128)S(1)} fusion(f32[64,512]{1,0:T(8,128)S(1)} %convert_add_fusion, f32[512]{0:T(512)S(1)} %copy-done.4, bf16[1,512,2304]{2,1,0:T(8,128)(2,1)S(1)} %copy-done.1), kind=kOutput, calls=%fused_computation.36 | convolution fusion | flops 75546624 | bytes 2721792 | tf_op jit(solution)/shard_map/dot_general | solution.py:72
  24.1 0.0 collective-permute-done.4
  24.1 0.0 collective-permute-done.5
  24.1 0.5 %fusion = bf16[32,2304]{1,0:T(8,128)(2,1)S(1)} fusion(f32[32,2304]{1,0:T(8,128)S(1)} %fusion.23, bf16[512,2304]{1,0:T(8,128)(2,1)S(1)} %collective-permute-done.5, f32[64,512]{1,0:T(8,128)S(1)} %convert_add_fusion, f32[512]{0:T(512)S(1)} %collective-permute-done.4), kind=kOutput, calls=%fused_computation.2 | convolution fusion | flops 75694080 | bytes 2869248 | tf_op jit(solution)/shard_map/dot_general | solution.py:72
  24.6 0.0 copy-start.3
  24.7 0.5 %convolution_add_fusion.1 = f32[32,2304]{1,0:T(8,128)S(1)} fusion(f32[32,2304]{1,0:T(8,128)S(1)} %fusion.20, bf16[512,2304]{1,0:T(8,128)(2,1)S(1)} %collective-permute-done.5, f32[64,512]{1,0:T(8,128)S(1)} %convert_add_fusion.2, f32[512]{0:T(512)S(1)} %collective-permute-done.4), kind=kOutput, calls=%fused_computation.1 | convolution fusion | flops 75620352 | bytes 3016704 | tf_op jit(solution)/shard_map/dot_general | solution.py:72
  25.2 0.1 collective-permute-start.6
  25.3 3.1 %collective-permute-start.11 = (bf16[16,2304]{1,0:T(8,128)(2,1)S(1)}, bf16[16,2304]{1,0:T(8,128)(2,1)S(1)}, u32[]{:S(2)}, u32[]{:S(2)}) collective-permute-start(bf16[16,2304]{1,0:T(8,128)(2,1)S(1)} %get-tuple-element.5), channel_id=1, source_target_pairs={{5,0},{4,1},{7,2},{6,3},{1,4},{0,5},{3,6},{2,7},{13,8},{12,9},{15,... | collective-permute-start | bytes 221192 | tf_op jit(solution)/shard_map/ppermute | solution.py:94
  28.4 0.8 %collective-permute-start.12 = (bf16[16,2304]{1,0:T(8,128)(2,1)S(1)}, bf16[16,2304]{1,0:T(8,128)(2,1)S(1)}, u32[]{:S(2)}, u32[]{:S(2)}) collective-permute-start(bf16[16,2304]{1,0:T(8,128)(2,1)S(1)} %get-tuple-element.6), channel_id=1, source_target_pairs={{3,0},{2,1},{1,2},{0,3},{7,4},{6,5},{5,6},{4,7},{11,8},{10,9},{9,1... | collective-permute-start | bytes 221192 | tf_op jit(solution)/shard_map/ppermute | solution.py:94
  29.2 0.0 copy-done.3
  29.2 2.4 %collective-permute-done.6 = bf16[16,2304]{1,0:T(8,128)(2,1)S(1)} collective-permute-done((bf16[16,2304]{1,0:T(8,128)(2,1)S(1)}, bf16[16,2304]{1,0:T(8,128)(2,1)S(1)}, u32[]{:S(2)}, u32[]{:S(2)}) %collective-permute-start.6) | collective-permute-done | bytes 73760 | tf_op jit(solution)/shard_map/ppermute | solution.py:89
  31.6 4.0 %collective-permute-done.11 = bf16[16,2304]{1,0:T(8,128)(2,1)S(1)} collective-permute-done((bf16[16,2304]{1,0:T(8,128)(2,1)S(1)}, bf16[16,2304]{1,0:T(8,128)(2,1)S(1)}, u32[]{:S(2)}, u32[]{:S(2)}) %collective-permute-start.11) | collective-permute-done | bytes 73760 | tf_op jit(solution)/shard_map/ppermute | solution.py:94
  35.6 0.0 collective-permute-done.12
  35.6 0.7 %fusion.9 = bf16[16,1,2304]{2,0,1:T(8,128)(2,1)} fusion(bf16[16,2304]{1,0:T(8,128)(2,1)S(1)} %collective-permute-done.12, bf16[16,2304]{1,0:T(8,128)(2,1)S(1)} %collective-permute-done.11, bf16[16,2304]{1,0:T(8,128)(2,1)S(1)} %collective-permute-done.6, f32[32,2304]{1,0:T(8,128)S(1)} %convolution_add_fusion.1, f32[2304]{0:T(1024)S(1)} %reduce), kind=kLoop, calls=%fused_computation.20 | loop fusion | flops 294912 | bytes 451584 | tf_op jit(solution)/shard_map/broadcast_in_dim | solution.py:99
  (11 shorter events, 0.2 us)
Async XLA Ops:
  0.0 11.8 %collective-permute-start.1 = (bf16[2304,512]{1,0:T(8,128)(2,1)}, bf16[2304,512]{1,0:T(8,128)(2,1)S(1)}, u32[]{:S(2)}, u32[]{:S(2)}) collective-permute-start(bf16[2304,512]{1,0:T(8,128)(2,1)} %bitcast.17), channel_id=1, source_target_pairs={{0,1},{1,0},{2,3},{3,2},{4,5},{5,4},{6,7},{7,6},{8,9},{9,8},{10,11... | collective-permute-start | bytes 7077896 | tf_op jit(solution)/shard_map/ppermute | solution.py:79
  0.5 7.8 %collective-permute-start.7 = (bf16[16,2304]{1,0:T(8,128)(2,1)}, bf16[16,2304]{1,0:T(8,128)(2,1)S(1)}, u32[]{:S(2)}, u32[]{:S(2)}) collective-permute-start(bf16[16,2304]{1,0:T(8,128)(2,1)} %bitcast.20), channel_id=1, source_target_pairs={{0,5},{1,4},{2,7},{3,6},{4,1},{5,0},{6,3},{7,2},{8,13},{9,12},{10,... | collective-permute-start | bytes 221192 | tf_op jit(solution)/shard_map/ppermute | solution.py:76
  4.2 5.0 %collective-permute-start.8 = (bf16[16,2304]{1,0:T(8,128)(2,1)}, bf16[16,2304]{1,0:T(8,128)(2,1)S(1)}, u32[]{:S(2)}, u32[]{:S(2)}) collective-permute-start(bf16[16,2304]{1,0:T(8,128)(2,1)} %bitcast.21), channel_id=1, source_target_pairs={{0,3},{1,2},{2,1},{3,0},{4,7},{5,6},{6,5},{7,4},{8,11},{9,10},{10,... | collective-permute-start | bytes 221192 | tf_op jit(solution)/shard_map/ppermute | solution.py:76
  5.4 5.9 %collective-permute-start = (bf16[16,2304]{1,0:T(8,128)(2,1)}, bf16[16,2304]{1,0:T(8,128)(2,1)S(1)}, u32[]{:S(2)}, u32[]{:S(2)}) collective-permute-start(bf16[16,2304]{1,0:T(8,128)(2,1)} %bitcast.22), channel_id=1, source_target_pairs={{0,7},{1,6},{2,5},{3,4},{4,3},{5,2},{6,1},{7,0},{8,15},{9,14},{10,... | collective-permute-start | bytes 221192 | tf_op jit(solution)/shard_map/ppermute | solution.py:76
  5.4 18.8 %collective-permute-start.4 = (f32[512]{0:T(512)}, f32[512]{0:T(512)S(1)}, u32[]{:S(2)}, u32[]{:S(2)}) collective-permute-start(f32[512]{0:T(512)} %param.7), channel_id=1, source_target_pairs={{0,1},{1,0},{2,3},{3,2},{4,5},{5,4},{6,7},{7,6},{8,9},{9,8},{10,11... | collective-permute-start | bytes 6152 | tf_op jit(solution)/shard_map/ppermute | solution.py:81
  5.9 1.7 %copy-start = (bf16[1,2304,512]{2,1,0:T(8,128)(2,1)S(1)}, bf16[1,2304,512]{2,1,0:T(8,128)(2,1)}, u32[]{:S(2)}) copy-start(bf16[1,2304,512]{2,1,0:T(8,128)(2,1)} %param.6) | copy-start | bytes 7077892
  7.5 1.7 %copy-start.1 = (bf16[1,512,2304]{2,1,0:T(8,128)(2,1)S(1)}, bf16[1,512,2304]{2,1,0:T(8,128)(2,1)}, u32[]{:S(2)}) copy-start(bf16[1,512,2304]{2,1,0:T(8,128)(2,1)} %param.8) | copy-start | bytes 7077892
  7.7 3.5 %copy-start.2 = (bf16[16,1,2304]{2,0,1:T(8,128)(2,1)S(1)}, bf16[16,1,2304]{2,0,1:T(8,128)(2,1)}, u32[]{:S(2)}) copy-start(bf16[16,1,2304]{2,0,1:T(8,128)(2,1)} %param.5) | copy-start | bytes 221188
  9.2 14.9 %collective-permute-start.5 = (bf16[512,2304]{1,0:T(8,128)(2,1)S(1)}, bf16[512,2304]{1,0:T(8,128)(2,1)S(1)}, u32[]{:S(2)}, u32[]{:S(2)}) collective-permute-start(bf16[512,2304]{1,0:T(8,128)(2,1)S(1)} %bitcast.19), channel_id=1, source_target_pairs={{0,1},{1,0},{2,3},{3,2},{4,5},{5,4},{6,7},{7,6},{8,9},{9,8},{10,11... | collective-permute-start | bytes 7077896 | tf_op jit(solution)/shard_map/ppermute | solution.py:80
  12.3 10.8 %copy-start.4 = (f32[512]{0:T(512)S(1)}, f32[512]{0:T(512)}, u32[]{:S(2)}) copy-start(f32[512]{0:T(512)} %param.7) | copy-start | bytes 6148
  12.3 4.6 %collective-permute-start.9 = (bf16[64,512]{1,0:T(8,128)(2,1)S(1)}, bf16[64,512]{1,0:T(8,128)(2,1)S(1)}, u32[]{:S(2)}, u32[]{:S(2)}) collective-permute-start(bf16[64,512]{1,0:T(8,128)(2,1)S(1)} %fusion.5), channel_id=1, source_target_pairs={{0,16},{8,24},{16,0},{24,8},{1,17},{9,25},{17,1},{25,9},{2,18},{10... | collective-permute-start | bytes 196616 | tf_op jit(solution)/shard_map/ppermute | solution.py:64
  14.4 4.3 %collective-permute-start.2 = (bf16[64,512]{1,0:T(8,128)(2,1)S(1)}, bf16[64,512]{1,0:T(8,128)(2,1)S(1)}, u32[]{:S(2)}, u32[]{:S(2)}) collective-permute-start(bf16[64,512]{1,0:T(8,128)(2,1)S(1)} %fusion.6), channel_id=1, source_target_pairs={{0,8},{8,0},{16,24},{24,16},{1,9},{9,1},{17,25},{25,17},{2,10},{10... | collective-permute-start | bytes 196616 | tf_op jit(solution)/shard_map/ppermute | solution.py:64
  16.9 4.3 %collective-permute-start.10 = (bf16[64,512]{1,0:T(8,128)(2,1)S(1)}, bf16[64,512]{1,0:T(8,128)(2,1)S(1)}, u32[]{:S(2)}, u32[]{:S(2)}) collective-permute-start(bf16[64,512]{1,0:T(8,128)(2,1)S(1)} %fusion.11), channel_id=1, source_target_pairs={{0,8},{8,0},{16,24},{24,16},{1,9},{9,1},{17,25},{25,17},{2,10},{10... | collective-permute-start | bytes 196616 | tf_op jit(solution)/shard_map/ppermute | solution.py:64
  18.8 4.3 %collective-permute-start.3 = (bf16[64,512]{1,0:T(8,128)(2,1)S(1)}, bf16[64,512]{1,0:T(8,128)(2,1)S(1)}, u32[]{:S(2)}, u32[]{:S(2)}) collective-permute-start(bf16[64,512]{1,0:T(8,128)(2,1)S(1)} %fusion.10), channel_id=1, source_target_pairs={{0,16},{8,24},{16,0},{24,8},{1,17},{9,25},{17,1},{25,9},{2,18},{10... | collective-permute-start | bytes 196616 | tf_op jit(solution)/shard_map/ppermute | solution.py:64
  24.6 4.5 %copy-start.3 = (f32[1,2304]{1,0:T(1,128)S(1)}, f32[1,2304]{1,0:T(1,128)}, u32[]{:S(2)}) copy-start(f32[1,2304]{1,0:T(1,128)} %param.9) | copy-start | bytes 27652
  25.2 6.4 %collective-permute-start.6 = (bf16[16,2304]{1,0:T(8,128)(2,1)S(1)}, bf16[16,2304]{1,0:T(8,128)(2,1)S(1)}, u32[]{:S(2)}, u32[]{:S(2)}) collective-permute-start(bf16[16,2304]{1,0:T(8,128)(2,1)S(1)} %slice.76), channel_id=1, source_target_pairs={{7,0},{6,1},{5,2},{4,3},{3,4},{2,5},{1,6},{0,7},{15,8},{14,9},{13,... | collective-permute-start | bytes 221192 | tf_op jit(solution)/shard_map/ppermute | solution.py:89
  25.3 10.3 %collective-permute-start.11 = (bf16[16,2304]{1,0:T(8,128)(2,1)S(1)}, bf16[16,2304]{1,0:T(8,128)(2,1)S(1)}, u32[]{:S(2)}, u32[]{:S(2)}) collective-permute-start(bf16[16,2304]{1,0:T(8,128)(2,1)S(1)} %get-tuple-element.5), channel_id=1, source_target_pairs={{5,0},{4,1},{7,2},{6,3},{1,4},{0,5},{3,6},{2,7},{13,8},{12,9},{15,... | collective-permute-start | bytes 221192 | tf_op jit(solution)/shard_map/ppermute | solution.py:94
  28.4 7.2 %collective-permute-start.12 = (bf16[16,2304]{1,0:T(8,128)(2,1)S(1)}, bf16[16,2304]{1,0:T(8,128)(2,1)S(1)}, u32[]{:S(2)}, u32[]{:S(2)}) collective-permute-start(bf16[16,2304]{1,0:T(8,128)(2,1)S(1)} %get-tuple-element.6), channel_id=1, source_target_pairs={{3,0},{2,1},{1,2},{0,3},{7,4},{6,5},{5,6},{4,7},{11,8},{10,9},{9,1... | collective-permute-start | bytes 221192 | tf_op jit(solution)/shard_map/ppermute | solution.py:94

commit v3 on v2

--- a/solution.py
+++ b/solution.py
@@ -22,18 +22,24 @@
 
 
 def staged(x):
-    def body(src, dst, sem):
-        copy = pltpu.make_async_copy(src, dst, sem)
-        copy.start()
-        copy.wait()
+    parts = 4 if x.shape[0] % 64 == 0 else 1
+    step = x.shape[0] // parts
+
+    def body(src, dst, sems):
+        spans = [pl.ds(p * step, step) for p in range(parts)]
+        copies = [pltpu.make_async_copy(src.at[s], dst.at[s], sems.at[p]) for p, s in enumerate(spans)]
+        for copy in copies:
+            copy.start()
+        for copy in copies:
+            copy.wait()
 
     return pl.pallas_call(
         body,
         out_shape=pltpu.VMEM(x.shape, x.dtype),
-        in_specs=[pl.BlockSpec(memory_space=pl.ANY)],
+        in_specs=[pl.BlockSpec(memory_space=pltpu.HBM)],
         out_specs=pl.BlockSpec(memory_space=pltpu.VMEM),
-        scratch_shapes=[pltpu.SemaphoreType.DMA],
-        compiler_params=pltpu.CompilerParams(vmem_limit_bytes=4 << 20),
+        scratch_shapes=[pltpu.SemaphoreType.DMA((parts,))],
+        compiler_params=pltpu.CompilerParams(vmem_limit_bytes=56 << 20),
     )(x)
 
 

time: 36.4 us -> 36.6 us (level)
  local copies, waits for them, and re-layouts: 2.59 us -> 0.06 us
  Pallas kernels: 0.17 us -> 1.63 us
  waiting for transfers between devices: 12.7 us -> 13.6 us
  starting transfers between devices: 15.8 us -> 16.2 us
    unnamed x11 -> x9, local copies, waits for them, and re-layouts: 2.56 us -> 0.03 us
    pallas_call x1, Pallas kernels: 0.17 us -> 1.63 us  [staged(): pl.pallas_call(body, out_shape=pltpu.VMEM(x.shape, x.dtype), in_specs=[pl...]
    ppermute x3, waiting for transfers between devices: 2.13 us -> 2.82 us  [on_device(): got = [lax.ppermute(own, 'latent', table) for table in rounds]]
    ppermute x1, starting transfers between devices: 0.01 us -> 0.51 us  [on_device(): dec_far = lax.ppermute(dec, 'latent', swap)]
  transfers between devices with their start and end apart: 13 -> 13, of which waited for: 8 -> 9; matrix products, arithmetic and copies ran while one was open for 9% -> 9% of each run, Pallas kernels for 0% -> 4%
where the time goes in v3:
time: 36.6 us; the launch traced here: 36.4 us
  starting transfers between devices  16.2 us (44%)
  waiting for transfers between devices  13.6 us (37%)
  matrix products  3.96 us (11%)
  Pallas kernels  1.63 us (4%)
  other arithmetic  0.82 us (2%)
    ppermute x4, starting transfers between devices, mix(): got = lax.ppermute(pre.astype(jnp.bfloat16), 'layer', table)  5.94 us
    ppermute x3, starting transfers between devices, on_device(): got = [lax.ppermute(own, 'latent', table) for table in rounds]  4.93 us
    ppermute x4, waiting for transfers between devices, mix(): got = lax.ppermute(pre.astype(jnp.bfloat16), 'layer', table)  4.27 us
    ppermute x2, waiting for transfers between devices, on_device(): lax.ppermute(out[k * rows:(k + 1) * rows], 'latent', reverse(table))  4.25 us
    ppermute x2, starting transfers between devices, on_device(): lax.ppermute(out[k * rows:(k + 1) * rows], 'latent', reverse(table))  3.84 us
    ppermute x3, waiting for transfers between devices, on_device(): got = [lax.ppermute(own, 'latent', table) for table in rounds]  2.82 us
    ppermute x1, waiting for transfers between devices, on_device(): lax.ppermute(out[(k + 1) * rows:(k + 2) * rows], 'latent', reverse(table))  2.24 us
    pallas_call x1, Pallas kernels, staged(): pl.pallas_call(body, out_shape=pltpu.VMEM(x.shape, x.dtype), in_specs=[pl...  1.63 us
  transfers between devices with their start and end apart: 13, of which 9 were waited for; matrix products, arithmetic and copies ran while one was open for 9% of the time, Pallas kernels for 4%

profile of v3, /device:TPU:0, one launch (start us, length us, event | category | flops | bytes accessed | tf_op | source)
XLA Modules:
  0.0 36.4 jit_solution(8943341827885815224)
XLA Ops:
  0.0 0.5 %collective-permute-start.1 = (bf16[2304,512]{1,0:T(8,128)(2,1)}, bf16[2304,512]{1,0:T(8,128)(2,1)S(1)}, u32[]{:S(2)}, u32[]{:S(2)}) collective-permute-start(bf16[2304,512]{1,0:T(8,128)(2,1)} %bitcast.18), channel_id=1, source_target_pairs={{0,1},{1,0},{2,3},{3,2},{4,5},{5,4},{6,7},{7,6},{8,9},{9,8},{10,11... | collective-permute-start | bytes 7077896 | tf_op jit(solution)/shard_map/ppermute | solution.py:85
  0.5 0.0 copy-start
  0.5 3.7 %collective-permute-start.7 = (bf16[16,2304]{1,0:T(8,128)(2,1)}, bf16[16,2304]{1,0:T(8,128)(2,1)S(1)}, u32[]{:S(2)}, u32[]{:S(2)}) collective-permute-start(bf16[16,2304]{1,0:T(8,128)(2,1)} %bitcast.20), channel_id=1, source_target_pairs={{0,5},{1,4},{2,7},{3,6},{4,1},{5,0},{6,3},{7,2},{8,13},{9,12},{10,... | collective-permute-start | bytes 221192 | tf_op jit(solution)/shard_map/ppermute | solution.py:82
  4.2 1.2 %collective-permute-start.8 = (bf16[16,2304]{1,0:T(8,128)(2,1)}, bf16[16,2304]{1,0:T(8,128)(2,1)S(1)}, u32[]{:S(2)}, u32[]{:S(2)}) collective-permute-start(bf16[16,2304]{1,0:T(8,128)(2,1)} %bitcast.21), channel_id=1, source_target_pairs={{0,3},{1,2},{2,1},{3,0},{4,7},{5,6},{6,5},{7,4},{8,11},{9,10},{10,... | collective-permute-start | bytes 221192 | tf_op jit(solution)/shard_map/ppermute | solution.py:82
  5.4 0.0 collective-permute-start
  5.4 0.4 %collective-permute-start.4 = (f32[512]{0:T(512)}, f32[512]{0:T(512)S(1)}, u32[]{:S(2)}, u32[]{:S(2)}) collective-permute-start(f32[512]{0:T(512)} %param.7), channel_id=1, source_target_pairs={{0,1},{1,0},{2,3},{3,2},{4,5},{5,4},{6,7},{7,6},{8,9},{9,8},{10,11... | collective-permute-start | bytes 6152 | tf_op jit(solution)/shard_map/ppermute | solution.py:87
  5.9 1.6 %shard_map.55 = bf16[2304,512]{1,0:T(8,128)(2,1)S(1)} custom-call(bf16[2304,512]{1,0:T(8,128)(2,1)} %bitcast.19), custom_call_target="tpu_custom_call" | custom-call | tf_op jit(solution)/shard_map/pallas_call | solution.py:36
  7.5 0.0 copy-start.1
  7.5 0.7 %collective-permute-done.7 = bf16[16,2304]{1,0:T(8,128)(2,1)S(1)} collective-permute-done((bf16[16,2304]{1,0:T(8,128)(2,1)}, bf16[16,2304]{1,0:T(8,128)(2,1)S(1)}, u32[]{:S(2)}, u32[]{:S(2)}) %collective-permute-start.7) | collective-permute-done | bytes 73760 | tf_op jit(solution)/shard_map/ppermute | solution.py:82
  8.2 0.0 copy-done
  8.2 0.5 %collective-permute-start.5 = (bf16[512,2304]{1,0:T(8,128)(2,1)S(1)}, bf16[512,2304]{1,0:T(8,128)(2,1)S(1)}, u32[]{:S(2)}, u32[]{:S(2)}) collective-permute-start(bf16[512,2304]{1,0:T(8,128)(2,1)S(1)} %bitcast.17), channel_id=1, source_target_pairs={{0,1},{1,0},{2,3},{3,2},{4,5},{5,4},{6,7},{7,6},{8,9},{9,8},{10,11... | collective-permute-start | bytes 7077896 | tf_op jit(solution)/shard_map/ppermute | solution.py:86
  8.7 0.5 %collective-permute-done.8 = bf16[16,2304]{1,0:T(8,128)(2,1)S(1)} collective-permute-done((bf16[16,2304]{1,0:T(8,128)(2,1)}, bf16[16,2304]{1,0:T(8,128)(2,1)S(1)}, u32[]{:S(2)}, u32[]{:S(2)}) %collective-permute-start.8) | collective-permute-done | bytes 73760 | tf_op jit(solution)/shard_map/ppermute | solution.py:82
  9.2 0.5 %fusion.43 = f32[32,512]{1,0:T(8,128)S(1)} fusion(bf16[32,2304]{1,0:T(8,128)(2,1)S(1)} %constant_dynamic-update-slice_fusion, bf16[2304,512]{1,0:T(8,128)(2,1)S(1)} %shard_map.55), kind=kOutput, calls=%fused_computation.56 | convolution fusion | flops 75497472 | bytes 2572288 | tf_op jit(solution)/shard_map/dot_general | solution.py:61
  9.7 1.7 %collective-permute-done = bf16[16,2304]{1,0:T(8,128)(2,1)S(1)} collective-permute-done((bf16[16,2304]{1,0:T(8,128)(2,1)}, bf16[16,2304]{1,0:T(8,128)(2,1)S(1)}, u32[]{:S(2)}, u32[]{:S(2)}) %collective-permute-start) | collective-permute-done | bytes 73760 | tf_op jit(solution)/shard_map/ppermute | solution.py:82
  11.4 0.0 copy-done.1
  11.4 0.5 %fusion.8 = f32[32,512]{1,0:T(8,128)S(1)} fusion(bf16[2304,512]{1,0:T(8,128)(2,1)S(1)} %shard_map.55, bf16[16,2304]{1,0:T(8,128)(2,1)S(1)} %collective-permute-done, bf16[16,2304]{1,0:T(8,128)(2,1)S(1)} %bitcast.23), kind=kOutput, calls=%fused_computation.19 | convolution fusion | flops 75792384 | bytes 2572288 | tf_op jit(solution)/shard_map/dot_general | solution.py:61
  11.9 0.0 collective-permute-done.1
  11.9 0.5 %fusion.44 = f32[32,512]{1,0:T(8,128)S(1)} fusion(bf16[32,2304]{1,0:T(8,128)(2,1)S(1)} %constant_dynamic-update-slice_fusion, bf16[2304,512]{1,0:T(8,128)(2,1)S(1)} %collective-permute-done.1), kind=kOutput, calls=%fused_computation.57 | convolution fusion | flops 75497472 | bytes 2572288 | tf_op jit(solution)/shard_map/dot_general | solution.py:62
  12.4 0.0 copy-start.3
  12.4 1.6 %collective-permute-start.9 = (bf16[64,512]{1,0:T(8,128)(2,1)S(1)}, bf16[64,512]{1,0:T(8,128)(2,1)S(1)}, u32[]{:S(2)}, u32[]{:S(2)}) collective-permute-start(bf16[64,512]{1,0:T(8,128)(2,1)S(1)} %fusion.5), channel_id=1, source_target_pairs={{0,16},{8,24},{16,0},{24,8},{1,17},{9,25},{17,1},{25,9},{2,18},{10... | collective-permute-start | bytes 196616 | tf_op jit(solution)/shard_map/ppermute | solution.py:70
  14.0 0.5 %fusion.7 = f32[32,512]{1,0:T(8,128)S(1)} fusion(bf16[2304,512]{1,0:T(8,128)(2,1)S(1)} %collective-permute-done.1, bf16[16,2304]{1,0:T(8,128)(2,1)S(1)} %collective-permute-done, bf16[16,2304]{1,0:T(8,128)(2,1)S(1)} %bitcast.24), kind=kOutput, calls=%fused_computation.18 | convolution fusion | flops 75792384 | bytes 2572288 | tf_op jit(solution)/shard_map/dot_general | solution.py:62
  14.5 1.6 %collective-permute-start.2 = (bf16[64,512]{1,0:T(8,128)(2,1)S(1)}, bf16[64,512]{1,0:T(8,128)(2,1)S(1)}, u32[]{:S(2)}, u32[]{:S(2)}) collective-permute-start(bf16[64,512]{1,0:T(8,128)(2,1)S(1)} %fusion.6), channel_id=1, source_target_pairs={{0,8},{8,0},{16,24},{24,16},{1,9},{9,1},{17,25},{25,17},{2,10},{10... | collective-permute-start | bytes 196616 | tf_op jit(solution)/shard_map/ppermute | solution.py:70
  16.1 0.8 %collective-permute-done.9 = bf16[64,512]{1,0:T(8,128)(2,1)S(1)} collective-permute-done((bf16[64,512]{1,0:T(8,128)(2,1)S(1)}, bf16[64,512]{1,0:T(8,128)(2,1)S(1)}, u32[]{:S(2)}, u32[]{:S(2)}) %collective-permute-start.9) | collective-permute-done | bytes 65568 | tf_op jit(solution)/shard_map/ppermute | solution.py:70
  17.0 1.6 %collective-permute-start.10 = (bf16[64,512]{1,0:T(8,128)(2,1)S(1)}, bf16[64,512]{1,0:T(8,128)(2,1)S(1)}, u32[]{:S(2)}, u32[]{:S(2)}) collective-permute-start(bf16[64,512]{1,0:T(8,128)(2,1)S(1)} %fusion.11), channel_id=1, source_target_pairs={{0,8},{8,0},{16,24},{24,16},{1,9},{9,1},{17,25},{25,17},{2,10},{10... | collective-permute-start | bytes 196616 | tf_op jit(solution)/shard_map/ppermute | solution.py:70
  18.5 0.4 collective-permute-done.2
  18.9 1.2 %collective-permute-start.3 = (bf16[64,512]{1,0:T(8,128)(2,1)S(1)}, bf16[64,512]{1,0:T(8,128)(2,1)S(1)}, u32[]{:S(2)}, u32[]{:S(2)}) collective-permute-start(bf16[64,512]{1,0:T(8,128)(2,1)S(1)} %fusion.10), channel_id=1, source_target_pairs={{0,16},{8,24},{16,0},{24,8},{1,17},{9,25},{17,1},{25,9},{2,18},{10... | collective-permute-start | bytes 196616 | tf_op jit(solution)/shard_map/ppermute | solution.py:70
  20.1 1.2 %collective-permute-done.10 = bf16[64,512]{1,0:T(8,128)(2,1)S(1)} collective-permute-done((bf16[64,512]{1,0:T(8,128)(2,1)S(1)}, bf16[64,512]{1,0:T(8,128)(2,1)S(1)}, u32[]{:S(2)}, u32[]{:S(2)}) %collective-permute-start.10) | collective-permute-done | bytes 65568 | tf_op jit(solution)/shard_map/ppermute | solution.py:70
  21.3 1.9 %collective-permute-done.3 = bf16[64,512]{1,0:T(8,128)(2,1)S(1)} collective-permute-done((bf16[64,512]{1,0:T(8,128)(2,1)S(1)}, bf16[64,512]{1,0:T(8,128)(2,1)S(1)}, u32[]{:S(2)}, u32[]{:S(2)}) %collective-permute-start.3) | collective-permute-done | bytes 65568 | tf_op jit(solution)/shard_map/ppermute | solution.py:70
  23.2 0.0 copy-done.3
  23.2 0.5 %fusion.20 = f32[32,2304]{1,0:T(8,128)S(1)} fusion(f32[64,512]{1,0:T(8,128)S(1)} %convert_add_fusion.2, f32[512]{0:T(512)S(1)} %copy-done.3, bf16[1,512,2304]{2,1,0:T(8,128)(2,1)S(1)} %copy-done), kind=kOutput, calls=%fused_computation.35 | convolution fusion | flops 75546624 | bytes 2721792 | tf_op jit(solution)/shard_map/dot_general | solution.py:78
  23.7 0.5 %fusion.23 = f32[32,2304]{1,0:T(8,128)S(1)} fusion(f32[64,512]{1,0:T(8,128)S(1)} %convert_add_fusion, f32[512]{0:T(512)S(1)} %copy-done.3, bf16[1,512,2304]{2,1,0:T(8,128)(2,1)S(1)} %copy-done), kind=kOutput, calls=%fused_computation.36 | convolution fusion | flops 75546624 | bytes 2721792 | tf_op jit(solution)/shard_map/dot_general | solution.py:78
  24.2 0.0 collective-permute-done.4
  24.2 0.0 collective-permute-done.5
  24.3 0.5 %fusion = bf16[32,2304]{1,0:T(8,128)(2,1)S(1)} fusion(f32[32,2304]{1,0:T(8,128)S(1)} %fusion.23, bf16[512,2304]{1,0:T(8,128)(2,1)S(1)} %collective-permute-done.5, f32[64,512]{1,0:T(8,128)S(1)} %convert_add_fusion, f32[512]{0:T(512)S(1)} %collective-permute-done.4), kind=kOutput, calls=%fused_computation.2 | convolution fusion | flops 75694080 | bytes 2869248 | tf_op jit(solution)/shard_map/dot_general | solution.py:78
  24.8 0.0 copy-start.2
  24.8 0.5 %convolution_add_fusion.1 = f32[32,2304]{1,0:T(8,128)S(1)} fusion(f32[32,2304]{1,0:T(8,128)S(1)} %fusion.20, bf16[512,2304]{1,0:T(8,128)(2,1)S(1)} %collective-permute-done.5, f32[64,512]{1,0:T(8,128)S(1)} %convert_add_fusion.2, f32[512]{0:T(512)S(1)} %collective-permute-done.4), kind=kOutput, calls=%fused_computation.1 | convolution fusion | flops 75620352 | bytes 3016704 | tf_op jit(solution)/shard_map/dot_general | solution.py:78
  25.3 0.1 collective-permute-start.6
  25.4 3.1 %collective-permute-start.11 = (bf16[16,2304]{1,0:T(8,128)(2,1)S(1)}, bf16[16,2304]{1,0:T(8,128)(2,1)S(1)}, u32[]{:S(2)}, u32[]{:S(2)}) collective-permute-start(bf16[16,2304]{1,0:T(8,128)(2,1)S(1)} %get-tuple-element.5), channel_id=1, source_target_pairs={{5,0},{4,1},{7,2},{6,3},{1,4},{0,5},{3,6},{2,7},{13,8},{12,9},{15,... | collective-permute-start | bytes 221192 | tf_op jit(solution)/shard_map/ppermute | solution.py:100
  28.4 0.8 %collective-permute-start.12 = (bf16[16,2304]{1,0:T(8,128)(2,1)S(1)}, bf16[16,2304]{1,0:T(8,128)(2,1)S(1)}, u32[]{:S(2)}, u32[]{:S(2)}) collective-permute-start(bf16[16,2304]{1,0:T(8,128)(2,1)S(1)} %get-tuple-element.6), channel_id=1, source_target_pairs={{3,0},{2,1},{1,2},{0,3},{7,4},{6,5},{5,6},{4,7},{11,8},{10,9},{9,1... | collective-permute-start | bytes 221192 | tf_op jit(solution)/shard_map/ppermute | solution.py:100
  29.2 0.0 copy-done.2
  29.3 2.2 %collective-permute-done.6 = bf16[16,2304]{1,0:T(8,128)(2,1)S(1)} collective-permute-done((bf16[16,2304]{1,0:T(8,128)(2,1)S(1)}, bf16[16,2304]{1,0:T(8,128)(2,1)S(1)}, u32[]{:S(2)}, u32[]{:S(2)}) %collective-permute-start.6) | collective-permute-done | bytes 73760 | tf_op jit(solution)/shard_map/ppermute | solution.py:95
  31.5 4.3 %collective-permute-done.11 = bf16[16,2304]{1,0:T(8,128)(2,1)S(1)} collective-permute-done((bf16[16,2304]{1,0:T(8,128)(2,1)S(1)}, bf16[16,2304]{1,0:T(8,128)(2,1)S(1)}, u32[]{:S(2)}, u32[]{:S(2)}) %collective-permute-start.11) | collective-permute-done | bytes 73760 | tf_op jit(solution)/shard_map/ppermute | solution.py:100
  35.8 0.0 collective-permute-done.12
  35.8 0.7 %fusion.9 = bf16[16,1,2304]{2,0,1:T(8,128)(2,1)} fusion(bf16[16,2304]{1,0:T(8,128)(2,1)S(1)} %collective-permute-done.12, bf16[16,2304]{1,0:T(8,128)(2,1)S(1)} %collective-permute-done.11, bf16[16,2304]{1,0:T(8,128)(2,1)S(1)} %collective-permute-done.6, f32[32,2304]{1,0:T(8,128)S(1)} %convolution_add_fusion.1, f32[2304]{0:T(1024)S(1)} %reduce), kind=kLoop, calls=%fused_computation.20 | loop fusion | flops 294912 | bytes 451584 | tf_op jit(solution)/shard_map/broadcast_in_dim | solution.py:105
  (11 shorter events, 0.2 us)
Async XLA Ops:
  0.0 11.9 %collective-permute-start.1 = (bf16[2304,512]{1,0:T(8,128)(2,1)}, bf16[2304,512]{1,0:T(8,128)(2,1)S(1)}, u32[]{:S(2)}, u32[]{:S(2)}) collective-permute-start(bf16[2304,512]{1,0:T(8,128)(2,1)} %bitcast.18), channel_id=1, source_target_pairs={{0,1},{1,0},{2,3},{3,2},{4,5},{5,4},{6,7},{7,6},{8,9},{9,8},{10,11... | collective-permute-start | bytes 7077896 | tf_op jit(solution)/shard_map/ppermute | solution.py:85
  0.5 7.7 %copy-start = (bf16[1,512,2304]{2,1,0:T(8,128)(2,1)S(1)}, bf16[1,512,2304]{2,1,0:T(8,128)(2,1)}, u32[]{:S(2)}) copy-start(bf16[1,512,2304]{2,1,0:T(8,128)(2,1)} %param.8) | copy-start | bytes 7077892
  0.5 7.7 %collective-permute-start.7 = (bf16[16,2304]{1,0:T(8,128)(2,1)}, bf16[16,2304]{1,0:T(8,128)(2,1)S(1)}, u32[]{:S(2)}, u32[]{:S(2)}) collective-permute-start(bf16[16,2304]{1,0:T(8,128)(2,1)} %bitcast.20), channel_id=1, source_target_pairs={{0,5},{1,4},{2,7},{3,6},{4,1},{5,0},{6,3},{7,2},{8,13},{9,12},{10,... | collective-permute-start | bytes 221192 | tf_op jit(solution)/shard_map/ppermute | solution.py:82
  4.2 5.0 %collective-permute-start.8 = (bf16[16,2304]{1,0:T(8,128)(2,1)}, bf16[16,2304]{1,0:T(8,128)(2,1)S(1)}, u32[]{:S(2)}, u32[]{:S(2)}) collective-permute-start(bf16[16,2304]{1,0:T(8,128)(2,1)} %bitcast.21), channel_id=1, source_target_pairs={{0,3},{1,2},{2,1},{3,0},{4,7},{5,6},{6,5},{7,4},{8,11},{9,10},{10,... | collective-permute-start | bytes 221192 | tf_op jit(solution)/shard_map/ppermute | solution.py:82
  5.4 5.9 %collective-permute-start = (bf16[16,2304]{1,0:T(8,128)(2,1)}, bf16[16,2304]{1,0:T(8,128)(2,1)S(1)}, u32[]{:S(2)}, u32[]{:S(2)}) collective-permute-start(bf16[16,2304]{1,0:T(8,128)(2,1)} %bitcast.22), channel_id=1, source_target_pairs={{0,7},{1,6},{2,5},{3,4},{4,3},{5,2},{6,1},{7,0},{8,15},{9,14},{10,... | collective-permute-start | bytes 221192 | tf_op jit(solution)/shard_map/ppermute | solution.py:82
  5.4 18.8 %collective-permute-start.4 = (f32[512]{0:T(512)}, f32[512]{0:T(512)S(1)}, u32[]{:S(2)}, u32[]{:S(2)}) collective-permute-start(f32[512]{0:T(512)} %param.7), channel_id=1, source_target_pairs={{0,1},{1,0},{2,3},{3,2},{4,5},{5,4},{6,7},{7,6},{8,9},{9,8},{10,11... | collective-permute-start | bytes 6152 | tf_op jit(solution)/shard_map/ppermute | solution.py:87
  7.5 3.9 %copy-start.1 = (bf16[16,1,2304]{2,0,1:T(8,128)(2,1)S(1)}, bf16[16,1,2304]{2,0,1:T(8,128)(2,1)}, u32[]{:S(2)}) copy-start(bf16[16,1,2304]{2,0,1:T(8,128)(2,1)} %param.5) | copy-start | bytes 221188
  8.2 16.0 %collective-permute-start.5 = (bf16[512,2304]{1,0:T(8,128)(2,1)S(1)}, bf16[512,2304]{1,0:T(8,128)(2,1)S(1)}, u32[]{:S(2)}, u32[]{:S(2)}) collective-permute-start(bf16[512,2304]{1,0:T(8,128)(2,1)S(1)} %bitcast.17), channel_id=1, source_target_pairs={{0,1},{1,0},{2,3},{3,2},{4,5},{5,4},{6,7},{7,6},{8,9},{9,8},{10,11... | collective-permute-start | bytes 7077896 | tf_op jit(solution)/shard_map/ppermute | solution.py:86
  12.4 10.8 %copy-start.3 = (f32[512]{0:T(512)S(1)}, f32[512]{0:T(512)}, u32[]{:S(2)}) copy-start(f32[512]{0:T(512)} %param.7) | copy-start | bytes 6148
  12.4 4.5 %collective-permute-start.9 = (bf16[64,512]{1,0:T(8,128)(2,1)S(1)}, bf16[64,512]{1,0:T(8,128)(2,1)S(1)}, u32[]{:S(2)}, u32[]{:S(2)}) collective-permute-start(bf16[64,512]{1,0:T(8,128)(2,1)S(1)} %fusion.5), channel_id=1, source_target_pairs={{0,16},{8,24},{16,0},{24,8},{1,17},{9,25},{17,1},{25,9},{2,18},{10... | collective-permute-start | bytes 196616 | tf_op jit(solution)/shard_map/ppermute | solution.py:70
  14.5 4.3 %collective-permute-start.2 = (bf16[64,512]{1,0:T(8,128)(2,1)S(1)}, bf16[64,512]{1,0:T(8,128)(2,1)S(1)}, u32[]{:S(2)}, u32[]{:S(2)}) collective-permute-start(bf16[64,512]{1,0:T(8,128)(2,1)S(1)} %fusion.6), channel_id=1, source_target_pairs={{0,8},{8,0},{16,24},{24,16},{1,9},{9,1},{17,25},{25,17},{2,10},{10... | collective-permute-start | bytes 196616 | tf_op jit(solution)/shard_map/ppermute | solution.py:70
  17.0 4.3 %collective-permute-start.10 = (bf16[64,512]{1,0:T(8,128)(2,1)S(1)}, bf16[64,512]{1,0:T(8,128)(2,1)S(1)}, u32[]{:S(2)}, u32[]{:S(2)}) collective-permute-start(bf16[64,512]{1,0:T(8,128)(2,1)S(1)} %fusion.11), channel_id=1, source_target_pairs={{0,8},{8,0},{16,24},{24,16},{1,9},{9,1},{17,25},{25,17},{2,10},{10... | collective-permute-start | bytes 196616 | tf_op jit(solution)/shard_map/ppermute | solution.py:70
  18.9 4.3 %collective-permute-start.3 = (bf16[64,512]{1,0:T(8,128)(2,1)S(1)}, bf16[64,512]{1,0:T(8,128)(2,1)S(1)}, u32[]{:S(2)}, u32[]{:S(2)}) collective-permute-start(bf16[64,512]{1,0:T(8,128)(2,1)S(1)} %fusion.10), channel_id=1, source_target_pairs={{0,16},{8,24},{16,0},{24,8},{1,17},{9,25},{17,1},{25,9},{2,18},{10... | collective-permute-start | bytes 196616 | tf_op jit(solution)/shard_map/ppermute | solution.py:70
  24.8 4.5 %copy-start.2 = (f32[1,2304]{1,0:T(1,128)S(1)}, f32[1,2304]{1,0:T(1,128)}, u32[]{:S(2)}) copy-start(f32[1,2304]{1,0:T(1,128)} %param.9) | copy-start | bytes 27652
  25.3 6.2 %collective-permute-start.6 = (bf16[16,2304]{1,0:T(8,128)(2,1)S(1)}, bf16[16,2304]{1,0:T(8,128)(2,1)S(1)}, u32[]{:S(2)}, u32[]{:S(2)}) collective-permute-start(bf16[16,2304]{1,0:T(8,128)(2,1)S(1)} %slice.76), channel_id=1, source_target_pairs={{7,0},{6,1},{5,2},{4,3},{3,4},{2,5},{1,6},{0,7},{15,8},{14,9},{13,... | collective-permute-start | bytes 221192 | tf_op jit(solution)/shard_map/ppermute | solution.py:95
  25.4 10.4 %collective-permute-start.11 = (bf16[16,2304]{1,0:T(8,128)(2,1)S(1)}, bf16[16,2304]{1,0:T(8,128)(2,1)S(1)}, u32[]{:S(2)}, u32[]{:S(2)}) collective-permute-start(bf16[16,2304]{1,0:T(8,128)(2,1)S(1)} %get-tuple-element.5), channel_id=1, source_target_pairs={{5,0},{4,1},{7,2},{6,3},{1,4},{0,5},{3,6},{2,7},{13,8},{12,9},{15,... | collective-permute-start | bytes 221192 | tf_op jit(solution)/shard_map/ppermute | solution.py:100
  28.4 7.3 %collective-permute-start.12 = (bf16[16,2304]{1,0:T(8,128)(2,1)S(1)}, bf16[16,2304]{1,0:T(8,128)(2,1)S(1)}, u32[]{:S(2)}, u32[]{:S(2)}) collective-permute-start(bf16[16,2304]{1,0:T(8,128)(2,1)S(1)} %get-tuple-element.6), channel_id=1, source_target_pairs={{3,0},{2,1},{1,2},{0,3},{7,4},{6,5},{5,6},{4,7},{11,8},{10,9},{9,1... | collective-permute-start | bytes 221192 | tf_op jit(solution)/shard_map/ppermute | solution.py:100

commit v4 on v3

v4 whole, which is shorter than its diff:
```python
import jax
import jax.numpy as jnp
from jax import lax
from jax.experimental import pallas as pl
from jax.experimental.pallas import tpu as pltpu
from jax.sharding import PartitionSpec as P


def meetings(count):
    chips = count // 2
    assert chips & (chips - 1) == 0
    return [[(i, i ^ (2 * k + 1)) for i in range(count)] for k in range(chips - 1, 0, -1)]


def doublings(count):
    assert count & (count - 1) == 0
    return [[(i, i ^ (1 << k)) for i in range(count)] for k in range(count.bit_length() - 1)]


def reverse(table):
    return [(j, i) for i, j in table]


def staged(x):
    parts = 4 if x.shape[0] % 64 == 0 else 1
    step = x.shape[0] // parts

    def body(src, dst, sems):
        spans = [pl.ds(p * step, step) for p in range(parts)]
        copies = [pltpu.make_async_copy(src.at[s], dst.at[s], sems.at[p]) for p, s in enumerate(spans)]
        for copy in copies:
            copy.start()
        for copy in copies:
            copy.wait()

    return pl.pallas_call(
        body,
        out_shape=pltpu.VMEM(x.shape, x.dtype),
        in_specs=[pl.BlockSpec(memory_space=pltpu.HBM)],
        out_specs=pl.BlockSpec(memory_space=pltpu.VMEM),
        scratch_shapes=[pltpu.SemaphoreType.DMA((parts,))],
        compiler_params=pltpu.CompilerParams(vmem_limit_bytes=56 << 20),
    )(x)


VMEM = pl.BlockSpec(memory_space=pltpu.VMEM)
FLOAT, HALF = jnp.float32, jnp.bfloat16


def product(x, w):
    return jnp.dot(x, w, preferred_element_type=FLOAT)


def encode_call(shards, near, far):
    count, rows, panel = len(shards), sum(x.shape[0] for x in shards), near.shape[1]

    def body(*refs):
        near_ref, far_ref, pre, sent = refs[count:]
        x = jnp.concatenate([ref[...] for ref in refs[:count]], axis=0)
        for p, w in enumerate((near_ref, far_ref)):
            y = product(x, w[...])
            pre[pl.ds(p * rows, rows), :] = y
            sent[pl.ds(p * rows, rows), :] = y.astype(HALF)

    shape = (2 * rows, panel)
    return pl.pallas_call(
        body,
        out_shape=[jax.ShapeDtypeStruct(shape, FLOAT), jax.ShapeDtypeStruct(shape, HALF)],
        in_specs=[VMEM] * (count + 2),
        out_specs=[VMEM] * 2,
        compiler_params=pltpu.CompilerParams(vmem_limit_bytes=16 << 20),
    )(*shards, near, far)


def decode_call(share, other, bias, bias_far, near, far, own, rows):
    half, width = share.shape[0] // 2, near.shape[1]
    kinds = [FLOAT] * own + [HALF] * (half // rows - own)

    def body(share_ref, other_ref, bias_ref, bias_far_ref, near_ref, far_ref, *outs):
        total = share_ref[...] + other_ref[...].astype(FLOAT)
        code = jnp.maximum(total[:half] + bias_ref[...], 0.0).astype(HALF)
        code_far = jnp.maximum(total[half:] + bias_far_ref[...], 0.0).astype(HALF)
        y = product(code, near_ref[...]) + product(code_far, far_ref[...])
        for i, out in enumerate(outs):
            out[...] = y[i * rows : (i + 1) * rows].astype(out.dtype)

    return pl.pallas_call(
        body,
        out_shape=[jax.ShapeDtypeStruct((rows, width), kind) for kind in kinds],
        in_specs=[VMEM] * 6,
        out_specs=[VMEM] * len(kinds),
        compiler_params=pltpu.CompilerParams(vmem_limit_bytes=16 << 20),
    )(share, other, bias[None, :], bias_far[None, :], near, far)


def make(mesh):
    latent, layer = mesh.shape["latent"], mesh.shape["layer"]
    swap = [(i, i ^ 1) for i in range(latent)]
    rounds = meetings(latent)
    steps = doublings(layer)
    cut = len(rounds) // 2

    def on_device(acts, enc_weight, enc_bias, dec_weight, dec_bias):
        own = acts[:, 0, :]
        rows = own.shape[0]

        def permute(x, axis, table):
            return lax.ppermute(x, axis, table)

        def encode(shards):
            return encode_call(shards, enc_near, enc_far)

        def mix(order, pre, sent):
            for k, table in enumerate(order):
                other = permute(sent, "layer", table)
                if k + 1 < len(order):
                    pre = pre + other.astype(FLOAT)
                    sent = pre.astype(HALF)
            return pre, other

        def decode(own_too, share, other):
            return decode_call(share, other, enc_bias, bias_far, dec, dec_far, own_too, rows)

        got = [permute(own, "latent", table) for table in rounds]
        enc = enc_weight[0]
        dec = dec_weight[0]
        enc_far = permute(enc, "latent", swap)
        dec_far = permute(dec, "latent", swap)
        bias_far = permute(enc_bias, "latent", swap)
        enc_near = staged(enc)
        first = mix(steps, *encode([own] + got[:cut]))
        second = mix(steps[::-1], *encode(got[cut:]))
        own_out, *out = decode(1, *first)
        acc = own_out + dec_bias
        back = [permute(out[k], "latent", reverse(table)) for k, table in enumerate(rounds[:cut])]
        out = decode(0, *second)
        back += [permute(out[k], "latent", reverse(table)) for k, table in enumerate(rounds[cut:])]
        for part in back:
            acc = acc + part.astype(jnp.float32)
        return acc.astype(jnp.bfloat16)[:, None, :]

    return on_device


def solution(mesh):
    return jax.shard_map(
        make(mesh),
        mesh=mesh,
        in_specs=(
            P("latent", "layer", None),
            P("layer", None, "latent"),
            P("latent"),
            P("layer", "latent", None),
            P("layer", None),
        ),
        out_specs=P("latent", "layer", None),
        check_vma=False,
    )
```

time: 36.6 us -> 31.9 us (0.87)
  matrix products: 3.96 us -> 0 us
  Pallas kernels: 1.63 us -> 5.24 us
  waiting for transfers between devices: 13.6 us -> 10.2 us
  starting transfers between devices: 16.2 us -> 15.6 us
    dot_general x8 -> x0, matrix products: 3.96 us -> none  [the longest x2 1 us: encode(): jnp.dot(tokens, enc_far, preferred_element_type=jnp.float32)]
    pallas_call x0 -> x4, Pallas kernels: none -> 3.6 us  [the longest x2 1.81 us: decode_call(): pl.pallas_call(body, out_shape=[jax.ShapeDtypeStruct((rows, width), kind)...]
    ppermute x13, waiting for transfers between devices: 13.6 us -> 10.2 us  [permute(): return lax.ppermute(x, axis, table)]
    ppermute x13, starting transfers between devices: 16.2 us -> 15.6 us  [permute(): return lax.ppermute(x, axis, table)]
  transfers between devices with their start and end apart: 13 -> 13, of which waited for: 9 -> 7; matrix products, arithmetic and copies ran while one was open for 9% -> 0% of each run, Pallas kernels for 4% -> 16%
where the time goes in v4:
time: 31.9 us; the launch traced here: 31.8 us
  starting transfers between devices  15.6 us (49%)
  waiting for transfers between devices  10.2 us (32%)
  Pallas kernels  5.24 us (16%)
  other arithmetic  0.75 us (2%)
    ppermute x13, starting transfers between devices, permute(): return lax.ppermute(x, axis, table)  15.6 us
    ppermute x13, waiting for transfers between devices, permute(): return lax.ppermute(x, axis, table)  10.2 us
    pallas_call x2, Pallas kernels, decode_call(): pl.pallas_call(body, out_shape=[jax.ShapeDtypeStruct((rows, width), kind)...  1.81 us
    pallas_call x2, Pallas kernels, encode_call(): pl.pallas_call(body, out_shape=[jax.ShapeDtypeStruct(shape, FLOAT), jax.S...  1.79 us
    pallas_call x1, Pallas kernels, staged(): pl.pallas_call(body, out_shape=pltpu.VMEM(x.shape, x.dtype), in_specs=[pl...  1.63 us
    broadcast_in_dim x1, other arithmetic, on_device(): return acc.astype(jnp.bfloat16)[:, None, :]  0.68 us
  transfers between devices with their start and end apart: 13, of which 7 were waited for; matrix products, arithmetic and copies ran while one was open for 0% of the time, Pallas kernels for 16%

profile of v4, /device:TPU:0, one launch (start us, length us, event | category | flops | bytes accessed | tf_op | source)
XLA Modules:
  0.0 31.8 jit_solution(9206742686397610972)
XLA Ops:
  0.0 0.5 %collective-permute-start.1 = (bf16[2304,512]{1,0:T(8,128)(2,1)}, bf16[2304,512]{1,0:T(8,128)(2,1)S(1)}, u32[]{:S(2)}, u32[]{:S(2)}) collective-permute-start(bf16[2304,512]{1,0:T(8,128)(2,1)} %bitcast.18), channel_id=1, source_target_pairs={{0,1},{1,0},{2,3},{3,2},{4,5},{5,4},{6,7},{7,6},{8,9},{9,8},{10,11... | collective-permute-start | bytes 7077896 | tf_op jit(solution)/shard_map/ppermute | solution.py:108
  0.5 0.0 collective-permute-start.5
  0.5 2.7 %collective-permute-start.8 = (bf16[16,2304]{1,0:T(8,128)(2,1)}, bf16[16,2304]{1,0:T(8,128)(2,1)S(1)}, u32[]{:S(2)}, u32[]{:S(2)}) collective-permute-start(bf16[16,2304]{1,0:T(8,128)(2,1)} %bitcast.10), channel_id=1, source_target_pairs={{0,3},{1,2},{2,1},{3,0},{4,7},{5,6},{6,5},{7,4},{8,11},{9,10},{10,... | collective-permute-start | bytes 221192 | tf_op jit(solution)/shard_map/ppermute | solution.py:108
  3.2 2.7 %collective-permute-start.7 = (bf16[16,2304]{1,0:T(8,128)(2,1)}, bf16[16,2304]{1,0:T(8,128)(2,1)S(1)}, u32[]{:S(2)}, u32[]{:S(2)}) collective-permute-start(bf16[16,2304]{1,0:T(8,128)(2,1)} %bitcast.11), channel_id=1, source_target_pairs={{0,5},{1,4},{2,7},{3,6},{4,1},{5,0},{6,3},{7,2},{8,13},{9,12},{10,... | collective-permute-start | bytes 221192 | tf_op jit(solution)/shard_map/ppermute | solution.py:108
  5.9 0.0 collective-permute-start
  5.9 1.6 %shard_map.55.refs_2_ = bf16[2304,512]{1,0:T(8,128)(2,1)S(1)} custom-call(bf16[2304,512]{1,0:T(8,128)(2,1)} %bitcast.19), custom_call_target="tpu_custom_call" | custom-call | tf_op jit(solution)/shard_map/pallas_call | solution.py:36
  7.5 0.0 copy-start.1
  7.5 0.0 collective-permute-done.8.refs_1_
  7.5 1.4 %collective-permute-done.7.refs_0_ = bf16[16,2304]{1,0:T(8,128)(2,1)S(1)} collective-permute-done((bf16[16,2304]{1,0:T(8,128)(2,1)}, bf16[16,2304]{1,0:T(8,128)(2,1)S(1)}, u32[]{:S(2)}, u32[]{:S(2)}) %collective-permute-start.7) | collective-permute-done | bytes 73760 | tf_op jit(solution)/shard_map/ppermute | solution.py:108
  8.9 0.0 collective-permute-done.1.refs_3_
  8.9 0.9 %shard_map.58 = (f32[64,512]{1,0:T(8,128)S(1)}, bf16[64,512]{1,0:T(8,128)(2,1)S(1)}) custom-call(bf16[16,2304]{1,0:T(8,128)(2,1)S(1)} %collective-permute-done.7.refs_0_, bf16[16,2304]{1,0:T(8,128)(2,1)S(1)} %collective-permute-done.8.refs_1_, bf16[2304,512]{1,0:T(8,128)(2,1)S(1)} %shard_map.55.refs_2_, bf16[2304,512]{1,0:T(8,128)(2,1)S(1)} %collective-permute-done.1.refs_3_), custom_call_target="tpu_custom_call" | custom-call | tf_op jit(solution)/shard_map/pallas_call | solution.py:66
  9.8 0.0 copy-start.2
  9.8 0.0 copy-start
  9.8 1.6 %collective-permute-start.9 = (bf16[64,512]{1,0:T(8,128)(2,1)S(1)}, bf16[64,512]{1,0:T(8,128)(2,1)S(1)}, u32[]{:S(2)}, u32[]{:S(2)}) collective-permute-start(bf16[64,512]{1,0:T(8,128)(2,1)S(1)} %get-tuple-element.18), channel_id=1, source_target_pairs={{0,16},{8,24},{16,0},{24,8},{1,17},{9,25},{17,1},{25,9},{2,18},{10... | collective-permute-start | bytes 196616 | tf_op jit(solution)/shard_map/ppermute | solution.py:108
  11.4 0.9 %collective-permute-done.refs_1_ = bf16[16,2304]{1,0:T(8,128)(2,1)S(1)} collective-permute-done((bf16[16,2304]{1,0:T(8,128)(2,1)}, bf16[16,2304]{1,0:T(8,128)(2,1)S(1)}, u32[]{:S(2)}, u32[]{:S(2)}) %collective-permute-start) | collective-permute-done | bytes 73760 | tf_op jit(solution)/shard_map/ppermute | solution.py:108
  12.3 0.0 copy-done.1
  12.3 0.9 %shard_map.56 = (f32[64,512]{1,0:T(8,128)S(1)}, bf16[64,512]{1,0:T(8,128)(2,1)S(1)}) custom-call(bf16[16,2304]{1,0:T(8,128)(2,1)S(1)} %bitcast.13, bf16[16,2304]{1,0:T(8,128)(2,1)S(1)} %collective-permute-done.refs_1_, bf16[2304,512]{1,0:T(8,128)(2,1)S(1)} %shard_map.55.refs_2_, bf16[2304,512]{1,0:T(8,128)(2,1)S(1)} %collective-permute-done.1.refs_3_), custom_call_target="tpu_custom_call" | custom-call | tf_op jit(solution)/shard_map/pallas_call | solution.py:66
  13.2 1.5 %collective-permute-start.2 = (bf16[64,512]{1,0:T(8,128)(2,1)S(1)}, bf16[64,512]{1,0:T(8,128)(2,1)S(1)}, u32[]{:S(2)}, u32[]{:S(2)}) collective-permute-start(bf16[64,512]{1,0:T(8,128)(2,1)S(1)} %get-tuple-element.14), channel_id=1, source_target_pairs={{0,8},{8,0},{16,24},{24,16},{1,9},{9,1},{17,25},{25,17},{2,10},{10... | collective-permute-start | bytes 196616 | tf_op jit(solution)/shard_map/ppermute | solution.py:108
  14.7 0.0 collective-permute-done.9
  14.7 1.1 %collective-permute-start.10 = (bf16[64,512]{1,0:T(8,128)(2,1)S(1)}, bf16[64,512]{1,0:T(8,128)(2,1)S(1)}, u32[]{:S(2)}, u32[]{:S(2)}) collective-permute-start(bf16[64,512]{1,0:T(8,128)(2,1)S(1)} %get-tuple-element.23), channel_id=1, source_target_pairs={{0,8},{8,0},{16,24},{24,16},{1,9},{9,1},{17,25},{25,17},{2,10},{10... | collective-permute-start | bytes 196616 | tf_op jit(solution)/shard_map/ppermute | solution.py:108
  15.8 1.9 %collective-permute-done.2 = bf16[64,512]{1,0:T(8,128)(2,1)S(1)} collective-permute-done((bf16[64,512]{1,0:T(8,128)(2,1)S(1)}, bf16[64,512]{1,0:T(8,128)(2,1)S(1)}, u32[]{:S(2)}, u32[]{:S(2)}) %collective-permute-start.2) | collective-permute-done | bytes 65568 | tf_op jit(solution)/shard_map/ppermute | solution.py:108
  17.8 1.4 %collective-permute-start.3 = (bf16[64,512]{1,0:T(8,128)(2,1)S(1)}, bf16[64,512]{1,0:T(8,128)(2,1)S(1)}, u32[]{:S(2)}, u32[]{:S(2)}) collective-permute-start(bf16[64,512]{1,0:T(8,128)(2,1)S(1)} %get-tuple-element.21), channel_id=1, source_target_pairs={{0,16},{8,24},{16,0},{24,8},{1,17},{9,25},{17,1},{25,9},{2,18},{10... | collective-permute-start | bytes 196616 | tf_op jit(solution)/shard_map/ppermute | solution.py:108
  19.1 0.0 copy-done.2
  19.1 0.0 collective-permute-start.4
  19.1 1.2 %collective-permute-done.4 = f32[512]{0:T(512)S(1)} collective-permute-done((f32[512]{0:T(512)S(1)}, f32[512]{0:T(512)S(1)}, u32[]{:S(2)}, u32[]{:S(2)}) %collective-permute-start.4) | collective-permute-done | bytes 2080 | tf_op jit(solution)/shard_map/ppermute | solution.py:108
  20.3 0.0 collective-permute-done.5.far_ref
  20.3 0.0 collective-permute-done.10.other_ref
  20.3 0.0 copy-done
  20.3 0.9 %shard_map.59 = (bf16[16,2304]{1,0:T(8,128)(2,1)S(1)}, bf16[16,2304]{1,0:T(8,128)(2,1)S(1)}) custom-call(f32[64,512]{1,0:T(8,128)S(1)} %get-tuple-element.24.share_ref, bf16[64,512]{1,0:T(8,128)(2,1)S(1)} %collective-permute-done.10.other_ref, f32[1,512]{1,0:T(1,128)S(1)} %bitcast.14, f32[1,512]{1,0:T(1,128)S(1)} %bitcast.16, bf16[512,2304]{1,0:T(8,128)(2,1)S(1)} %bitcast.8, ...), custom_call_target="tpu_custom_call" | custom-call | tf_op jit(solution)/shard_map/pallas_call | solution.py:87
  21.2 2.3 %collective-permute-start.11 = (bf16[16,2304]{1,0:T(8,128)(2,1)S(1)}, bf16[16,2304]{1,0:T(8,128)(2,1)S(1)}, u32[]{:S(2)}, u32[]{:S(2)}) collective-permute-start(bf16[16,2304]{1,0:T(8,128)(2,1)S(1)} %get-tuple-element.19), channel_id=1, source_target_pairs={{5,0},{4,1},{7,2},{6,3},{1,4},{0,5},{3,6},{2,7},{13,8},{12,9},{15,... | collective-permute-start | bytes 221192 | tf_op jit(solution)/shard_map/ppermute | solution.py:108
  23.5 0.8 %collective-permute-start.12 = (bf16[16,2304]{1,0:T(8,128)(2,1)S(1)}, bf16[16,2304]{1,0:T(8,128)(2,1)S(1)}, u32[]{:S(2)}, u32[]{:S(2)}) collective-permute-start(bf16[16,2304]{1,0:T(8,128)(2,1)S(1)} %get-tuple-element.20), channel_id=1, source_target_pairs={{3,0},{2,1},{1,2},{0,3},{7,4},{6,5},{5,6},{4,7},{11,8},{10,9},{9,1... | collective-permute-start | bytes 221192 | tf_op jit(solution)/shard_map/ppermute | solution.py:108
  24.2 0.0 collective-permute-done.3.other_ref
  24.2 0.0 copy-start.3
  24.2 0.9 %shard_map.57 = (f32[16,2304]{1,0:T(8,128)S(1)}, bf16[16,2304]{1,0:T(8,128)(2,1)S(1)}) custom-call(f32[64,512]{1,0:T(8,128)S(1)} %get-tuple-element.22.share_ref, bf16[64,512]{1,0:T(8,128)(2,1)S(1)} %collective-permute-done.3.other_ref, f32[1,512]{1,0:T(1,128)S(1)} %bitcast.15, f32[1,512]{1,0:T(1,128)S(1)} %bitcast.17, bf16[512,2304]{1,0:T(8,128)(2,1)S(1)} %bitcast.9, ...), custom_call_target="tpu_custom_call" | custom-call | tf_op jit(solution)/shard_map/pallas_call | solution.py:87
  25.1 1.1 %collective-permute-start.6 = (bf16[16,2304]{1,0:T(8,128)(2,1)S(1)}, bf16[16,2304]{1,0:T(8,128)(2,1)S(1)}, u32[]{:S(2)}, u32[]{:S(2)}) collective-permute-start(bf16[16,2304]{1,0:T(8,128)(2,1)S(1)} %get-tuple-element.16), channel_id=1, source_target_pairs={{7,0},{6,1},{5,2},{4,3},{3,4},{2,5},{1,6},{0,7},{15,8},{14,9},{13,... | collective-permute-start | bytes 221192 | tf_op jit(solution)/shard_map/ppermute | solution.py:108
  26.3 0.0 copy-done.3
  26.3 0.1 collective-permute-done.11
  26.4 1.5 %collective-permute-done.12 = bf16[16,2304]{1,0:T(8,128)(2,1)S(1)} collective-permute-done((bf16[16,2304]{1,0:T(8,128)(2,1)S(1)}, bf16[16,2304]{1,0:T(8,128)(2,1)S(1)}, u32[]{:S(2)}, u32[]{:S(2)}) %collective-permute-start.12) | collective-permute-done | bytes 73760 | tf_op jit(solution)/shard_map/ppermute | solution.py:108
  27.9 3.2 %collective-permute-done.6 = bf16[16,2304]{1,0:T(8,128)(2,1)S(1)} collective-permute-done((bf16[16,2304]{1,0:T(8,128)(2,1)S(1)}, bf16[16,2304]{1,0:T(8,128)(2,1)S(1)}, u32[]{:S(2)}, u32[]{:S(2)}) %collective-permute-start.6) | collective-permute-done | bytes 73760 | tf_op jit(solution)/shard_map/ppermute | solution.py:108
  31.1 0.7 %fusion = bf16[16,1,2304]{2,0,1:T(8,128)(2,1)} fusion(bf16[16,2304]{1,0:T(8,128)(2,1)S(1)} %collective-permute-done.12, bf16[16,2304]{1,0:T(8,128)(2,1)S(1)} %collective-permute-done.11, bf16[16,2304]{1,0:T(8,128)(2,1)S(1)} %collective-permute-done.6, f32[16,2304]{1,0:T(8,128)S(1)} %get-tuple-element.15, f32[2304]{0:T(1024)S(1)} %reduce), kind=kLoop, calls=%fused_computation.3 | loop fusion | flops 294912 | bytes 451584 | tf_op jit(solution)/shard_map/broadcast_in_dim | solution.py:140
  (3 shorter events, 0.1 us)
Async XLA Ops:
  0.0 8.9 %collective-permute-start.1 = (bf16[2304,512]{1,0:T(8,128)(2,1)}, bf16[2304,512]{1,0:T(8,128)(2,1)S(1)}, u32[]{:S(2)}, u32[]{:S(2)}) collective-permute-start(bf16[2304,512]{1,0:T(8,128)(2,1)} %bitcast.18), channel_id=1, source_target_pairs={{0,1},{1,0},{2,3},{3,2},{4,5},{5,4},{6,7},{7,6},{8,9},{9,8},{10,11... | collective-permute-start | bytes 7077896 | tf_op jit(solution)/shard_map/ppermute | solution.py:108
  0.5 19.8 %collective-permute-start.5 = (bf16[512,2304]{1,0:T(8,128)(2,1)}, bf16[512,2304]{1,0:T(8,128)(2,1)S(1)}, u32[]{:S(2)}, u32[]{:S(2)}) collective-permute-start(bf16[512,2304]{1,0:T(8,128)(2,1)} %bitcast.7), channel_id=1, source_target_pairs={{0,1},{1,0},{2,3},{3,2},{4,5},{5,4},{6,7},{7,6},{8,9},{9,8},{10,11... | collective-permute-start | bytes 7077896 | tf_op jit(solution)/shard_map/ppermute | solution.py:108
  0.5 7.0 %collective-permute-start.8 = (bf16[16,2304]{1,0:T(8,128)(2,1)}, bf16[16,2304]{1,0:T(8,128)(2,1)S(1)}, u32[]{:S(2)}, u32[]{:S(2)}) collective-permute-start(bf16[16,2304]{1,0:T(8,128)(2,1)} %bitcast.10), channel_id=1, source_target_pairs={{0,3},{1,2},{2,1},{3,0},{4,7},{5,6},{6,5},{7,4},{8,11},{9,10},{10,... | collective-permute-start | bytes 221192 | tf_op jit(solution)/shard_map/ppermute | solution.py:108
  3.2 5.7 %collective-permute-start.7 = (bf16[16,2304]{1,0:T(8,128)(2,1)}, bf16[16,2304]{1,0:T(8,128)(2,1)S(1)}, u32[]{:S(2)}, u32[]{:S(2)}) collective-permute-start(bf16[16,2304]{1,0:T(8,128)(2,1)} %bitcast.11), channel_id=1, source_target_pairs={{0,5},{1,4},{2,7},{3,6},{4,1},{5,0},{6,3},{7,2},{8,13},{9,12},{10,... | collective-permute-start | bytes 221192 | tf_op jit(solution)/shard_map/ppermute | solution.py:108
  5.9 6.4 %collective-permute-start = (bf16[16,2304]{1,0:T(8,128)(2,1)}, bf16[16,2304]{1,0:T(8,128)(2,1)S(1)}, u32[]{:S(2)}, u32[]{:S(2)}) collective-permute-start(bf16[16,2304]{1,0:T(8,128)(2,1)} %bitcast.12), channel_id=1, source_target_pairs={{0,7},{1,6},{2,5},{3,4},{4,3},{5,2},{6,1},{7,0},{8,15},{9,14},{10,... | collective-permute-start | bytes 221192 | tf_op jit(solution)/shard_map/ppermute | solution.py:108
  7.5 4.8 %copy-start.1 = (bf16[16,1,2304]{2,0,1:T(8,128)(2,1)S(1)}, bf16[16,1,2304]{2,0,1:T(8,128)(2,1)}, u32[]{:S(2)}) copy-start(bf16[16,1,2304]{2,0,1:T(8,128)(2,1)} %param.5) | copy-start | bytes 221188
  9.8 9.4 %copy-start.2 = (f32[512]{0:T(512)S(1)}, f32[512]{0:T(512)}, u32[]{:S(2)}) copy-start(f32[512]{0:T(512)} %param.7) | copy-start | bytes 6148
  9.8 10.5 %copy-start = (bf16[1,512,2304]{2,1,0:T(8,128)(2,1)S(1)}, bf16[1,512,2304]{2,1,0:T(8,128)(2,1)}, u32[]{:S(2)}) copy-start(bf16[1,512,2304]{2,1,0:T(8,128)(2,1)} %param.8) | copy-start | bytes 7077892
  9.8 4.9 %collective-permute-start.9 = (bf16[64,512]{1,0:T(8,128)(2,1)S(1)}, bf16[64,512]{1,0:T(8,128)(2,1)S(1)}, u32[]{:S(2)}, u32[]{:S(2)}) collective-permute-start(bf16[64,512]{1,0:T(8,128)(2,1)S(1)} %get-tuple-element.18), channel_id=1, source_target_pairs={{0,16},{8,24},{16,0},{24,8},{1,17},{9,25},{17,1},{25,9},{2,18},{10... | collective-permute-start | bytes 196616 | tf_op jit(solution)/shard_map/ppermute | solution.py:108
  13.2 4.6 %collective-permute-start.2 = (bf16[64,512]{1,0:T(8,128)(2,1)S(1)}, bf16[64,512]{1,0:T(8,128)(2,1)S(1)}, u32[]{:S(2)}, u32[]{:S(2)}) collective-permute-start(bf16[64,512]{1,0:T(8,128)(2,1)S(1)} %get-tuple-element.14), channel_id=1, source_target_pairs={{0,8},{8,0},{16,24},{24,16},{1,9},{9,1},{17,25},{25,17},{2,10},{10... | collective-permute-start | bytes 196616 | tf_op jit(solution)/shard_map/ppermute | solution.py:108
  14.7 5.6 %collective-permute-start.10 = (bf16[64,512]{1,0:T(8,128)(2,1)S(1)}, bf16[64,512]{1,0:T(8,128)(2,1)S(1)}, u32[]{:S(2)}, u32[]{:S(2)}) collective-permute-start(bf16[64,512]{1,0:T(8,128)(2,1)S(1)} %get-tuple-element.23), channel_id=1, source_target_pairs={{0,8},{8,0},{16,24},{24,16},{1,9},{9,1},{17,25},{25,17},{2,10},{10... | collective-permute-start | bytes 196616 | tf_op jit(solution)/shard_map/ppermute | solution.py:108
  17.8 6.5 %collective-permute-start.3 = (bf16[64,512]{1,0:T(8,128)(2,1)S(1)}, bf16[64,512]{1,0:T(8,128)(2,1)S(1)}, u32[]{:S(2)}, u32[]{:S(2)}) collective-permute-start(bf16[64,512]{1,0:T(8,128)(2,1)S(1)} %get-tuple-element.21), channel_id=1, source_target_pairs={{0,16},{8,24},{16,0},{24,8},{1,17},{9,25},{17,1},{25,9},{2,18},{10... | collective-permute-start | bytes 196616 | tf_op jit(solution)/shard_map/ppermute | solution.py:108
  19.1 1.2 %collective-permute-start.4 = (f32[512]{0:T(512)S(1)}, f32[512]{0:T(512)S(1)}, u32[]{:S(2)}, u32[]{:S(2)}) collective-permute-start(f32[512]{0:T(512)S(1)} %copy-done.2), channel_id=1, source_target_pairs={{0,1},{1,0},{2,3},{3,2},{4,5},{5,4},{6,7},{7,6},{8,9},{9,8},{10,11... | collective-permute-start | bytes 6152 | tf_op jit(solution)/shard_map/ppermute | solution.py:108
  21.2 5.1 %collective-permute-start.11 = (bf16[16,2304]{1,0:T(8,128)(2,1)S(1)}, bf16[16,2304]{1,0:T(8,128)(2,1)S(1)}, u32[]{:S(2)}, u32[]{:S(2)}) collective-permute-start(bf16[16,2304]{1,0:T(8,128)(2,1)S(1)} %get-tuple-element.19), channel_id=1, source_target_pairs={{5,0},{4,1},{7,2},{6,3},{1,4},{0,5},{3,6},{2,7},{13,8},{12,9},{15,... | collective-permute-start | bytes 221192 | tf_op jit(solution)/shard_map/ppermute | solution.py:108
  23.5 4.4 %collective-permute-start.12 = (bf16[16,2304]{1,0:T(8,128)(2,1)S(1)}, bf16[16,2304]{1,0:T(8,128)(2,1)S(1)}, u32[]{:S(2)}, u32[]{:S(2)}) collective-permute-start(bf16[16,2304]{1,0:T(8,128)(2,1)S(1)} %get-tuple-element.20), channel_id=1, source_target_pairs={{3,0},{2,1},{1,2},{0,3},{7,4},{6,5},{5,6},{4,7},{11,8},{10,9},{9,1... | collective-permute-start | bytes 221192 | tf_op jit(solution)/shard_map/ppermute | solution.py:108
  24.2 2.0 %copy-start.3 = (f32[1,2304]{1,0:T(1,128)S(1)}, f32[1,2304]{1,0:T(1,128)}, u32[]{:S(2)}) copy-start(f32[1,2304]{1,0:T(1,128)} %param.9) | copy-start | bytes 27652
  25.1 6.0 %collective-permute-start.6 = (bf16[16,2304]{1,0:T(8,128)(2,1)S(1)}, bf16[16,2304]{1,0:T(8,128)(2,1)S(1)}, u32[]{:S(2)}, u32[]{:S(2)}) collective-permute-start(bf16[16,2304]{1,0:T(8,128)(2,1)S(1)} %get-tuple-element.16), channel_id=1, source_target_pairs={{7,0},{6,1},{5,2},{4,3},{3,4},{2,5},{1,6},{0,7},{15,8},{14,9},{13,... | collective-permute-start | bytes 221192 | tf_op jit(solution)/shard_map/ppermute | solution.py:108

commit v5 on v4

--- a/solution.py
+++ b/solution.py
@@ -93,6 +93,35 @@
     )(share, other, bias[None, :], bias_far[None, :], near, far)
 
 
+def finish_call(own, bias, parts):
+    rows, width = own.shape
+    blocks = 3 if width % 384 == 0 else 1
+    block, count = width // blocks, len(parts)
+
+    def body(own_ref, bias_ref, *refs):
+        out, held, sems = refs[count:]
+        copies = []
+        for b in range(blocks):
+            span = pl.ds(b * block, block)
+            total = own_ref[:, span] + bias_ref[:, span]
+            for ref in refs[:count]:
+                total = total + ref[:, span].astype(FLOAT)
+            held[:, span] = total.astype(HALF)
+            copies.append(pltpu.make_async_copy(held.at[:, span], out.at[:, span], sems.at[b]))
+            copies[-1].start()
+        for copy in copies:
+            copy.wait()
+
+    return pl.pallas_call(
+        body,
+        out_shape=jax.ShapeDtypeStruct((rows, width), HALF),
+        in_specs=[VMEM] * (2 + count),
+        out_specs=pl.BlockSpec(memory_space=pltpu.HBM),
+        scratch_shapes=[pltpu.VMEM((rows, width), HALF), pltpu.SemaphoreType.DMA((blocks,))],
+        compiler_params=pltpu.CompilerParams(vmem_limit_bytes=8 << 20),
+    )(own, bias, *parts)
+
+
 def make(mesh):
     latent, layer = mesh.shape["latent"], mesh.shape["layer"]
     swap = [(i, i ^ 1) for i in range(latent)]
@@ -131,13 +160,10 @@
         first = mix(steps, *encode([own] + got[:cut]))
         second = mix(steps[::-1], *encode(got[cut:]))
         own_out, *out = decode(1, *first)
-        acc = own_out + dec_bias
         back = [permute(out[k], "latent", reverse(table)) for k, table in enumerate(rounds[:cut])]
         out = decode(0, *second)
         back += [permute(out[k], "latent", reverse(table)) for k, table in enumerate(rounds[cut:])]
-        for part in back:
-            acc = acc + part.astype(jnp.float32)
-        return acc.astype(jnp.bfloat16)[:, None, :]
+        return finish_call(own_out, dec_bias, back)[:, None, :]
 
     return on_device
 

time: 31.9 us -> 31.9 us (level)
  other arithmetic: 0.75 us -> 0.03 us
  Pallas kernels: 5.24 us -> 5.92 us
    pallas_call x0 -> x1, Pallas kernels: none -> 0.68 us  [finish_call(): pl.pallas_call(body, out_shape=jax.ShapeDtypeStruct((rows, width), HALF),...]
    broadcast_in_dim x1 -> x0, other arithmetic: 0.68 us -> none  [on_device(): return acc.astype(jnp.bfloat16)[:, None, :]]
where the time goes in v5:
time: 31.9 us; the launch traced here: 31.8 us
  starting transfers between devices  15.6 us (49%)
  waiting for transfers between devices  10.2 us (32%)
  Pallas kernels  5.92 us (19%)
    ppermute x13, starting transfers between devices, permute(): return lax.ppermute(x, axis, table)  15.6 us
    ppermute x13, waiting for transfers between devices, permute(): return lax.ppermute(x, axis, table)  10.2 us
    pallas_call x2, Pallas kernels, decode_call(): pl.pallas_call(body, out_shape=[jax.ShapeDtypeStruct((rows, width), kind)...  1.81 us
    pallas_call x2, Pallas kernels, encode_call(): pl.pallas_call(body, out_shape=[jax.ShapeDtypeStruct(shape, FLOAT), jax.S...  1.79 us
    pallas_call x1, Pallas kernels, staged(): pl.pallas_call(body, out_shape=pltpu.VMEM(x.shape, x.dtype), in_specs=[pl...  1.63 us
    pallas_call x1, Pallas kernels, finish_call(): pl.pallas_call(body, out_shape=jax.ShapeDtypeStruct((rows, width), HALF),...  0.68 us
  transfers between devices with their start and end apart: 13, of which 7 were waited for; matrix products, arithmetic and copies ran while one was open for 0% of the time, Pallas kernels for 16%

profile of v5, /device:TPU:0, one launch (start us, length us, event | category | flops | bytes accessed | tf_op | source)
XLA Modules:
  0.0 31.8 jit_solution(10443037295409750812)
XLA Ops:
  0.0 0.5 %collective-permute-start.1 = (bf16[2304,512]{1,0:T(8,128)(2,1)}, bf16[2304,512]{1,0:T(8,128)(2,1)S(1)}, u32[]{:S(2)}, u32[]{:S(2)}) collective-permute-start(bf16[2304,512]{1,0:T(8,128)(2,1)} %bitcast.17), channel_id=1, source_target_pairs={{0,1},{1,0},{2,3},{3,2},{4,5},{5,4},{6,7},{7,6},{8,9},{9,8},{10,11... | collective-permute-start | bytes 7077896 | tf_op jit(solution)/shard_map/ppermute | solution.py:137
  0.5 0.0 collective-permute-start.5
  0.5 2.7 %collective-permute-start.8 = (bf16[16,2304]{1,0:T(8,128)(2,1)}, bf16[16,2304]{1,0:T(8,128)(2,1)S(1)}, u32[]{:S(2)}, u32[]{:S(2)}) collective-permute-start(bf16[16,2304]{1,0:T(8,128)(2,1)} %bitcast.9), channel_id=1, source_target_pairs={{0,3},{1,2},{2,1},{3,0},{4,7},{5,6},{6,5},{7,4},{8,11},{9,10},{10,... | collective-permute-start | bytes 221192 | tf_op jit(solution)/shard_map/ppermute | solution.py:137
  3.2 2.7 %collective-permute-start.7 = (bf16[16,2304]{1,0:T(8,128)(2,1)}, bf16[16,2304]{1,0:T(8,128)(2,1)S(1)}, u32[]{:S(2)}, u32[]{:S(2)}) collective-permute-start(bf16[16,2304]{1,0:T(8,128)(2,1)} %bitcast.10), channel_id=1, source_target_pairs={{0,5},{1,4},{2,7},{3,6},{4,1},{5,0},{6,3},{7,2},{8,13},{9,12},{10,... | collective-permute-start | bytes 221192 | tf_op jit(solution)/shard_map/ppermute | solution.py:137
  5.9 0.0 collective-permute-start
  5.9 1.6 %shard_map.55.refs_2_ = bf16[2304,512]{1,0:T(8,128)(2,1)S(1)} custom-call(bf16[2304,512]{1,0:T(8,128)(2,1)} %bitcast.18), custom_call_target="tpu_custom_call" | custom-call | tf_op jit(solution)/shard_map/pallas_call | solution.py:36
  7.5 0.0 copy-start.1
  7.5 0.0 collective-permute-done.8.refs_1_
  7.5 1.4 %collective-permute-done.7.refs_0_ = bf16[16,2304]{1,0:T(8,128)(2,1)S(1)} collective-permute-done((bf16[16,2304]{1,0:T(8,128)(2,1)}, bf16[16,2304]{1,0:T(8,128)(2,1)S(1)}, u32[]{:S(2)}, u32[]{:S(2)}) %collective-permute-start.7) | collective-permute-done | bytes 73760 | tf_op jit(solution)/shard_map/ppermute | solution.py:137
  8.9 0.0 collective-permute-done.1.refs_3_
  8.9 0.9 %shard_map.58 = (f32[64,512]{1,0:T(8,128)S(1)}, bf16[64,512]{1,0:T(8,128)(2,1)S(1)}) custom-call(bf16[16,2304]{1,0:T(8,128)(2,1)S(1)} %collective-permute-done.7.refs_0_, bf16[16,2304]{1,0:T(8,128)(2,1)S(1)} %collective-permute-done.8.refs_1_, bf16[2304,512]{1,0:T(8,128)(2,1)S(1)} %shard_map.55.refs_2_, bf16[2304,512]{1,0:T(8,128)(2,1)S(1)} %collective-permute-done.1.refs_3_), custom_call_target="tpu_custom_call" | custom-call | tf_op jit(solution)/shard_map/pallas_call | solution.py:66
  9.8 0.0 copy-start.3
  9.8 0.0 copy-start
  9.8 1.6 %collective-permute-start.9 = (bf16[64,512]{1,0:T(8,128)(2,1)S(1)}, bf16[64,512]{1,0:T(8,128)(2,1)S(1)}, u32[]{:S(2)}, u32[]{:S(2)}) collective-permute-start(bf16[64,512]{1,0:T(8,128)(2,1)S(1)} %get-tuple-element.18), channel_id=1, source_target_pairs={{0,16},{8,24},{16,0},{24,8},{1,17},{9,25},{17,1},{25,9},{2,18},{10... | collective-permute-start | bytes 196616 | tf_op jit(solution)/shard_map/ppermute | solution.py:137
  11.4 0.9 %collective-permute-done.refs_1_ = bf16[16,2304]{1,0:T(8,128)(2,1)S(1)} collective-permute-done((bf16[16,2304]{1,0:T(8,128)(2,1)}, bf16[16,2304]{1,0:T(8,128)(2,1)S(1)}, u32[]{:S(2)}, u32[]{:S(2)}) %collective-permute-start) | collective-permute-done | bytes 73760 | tf_op jit(solution)/shard_map/ppermute | solution.py:137
  12.3 0.0 copy-done.1
  12.3 0.9 %shard_map.56 = (f32[64,512]{1,0:T(8,128)S(1)}, bf16[64,512]{1,0:T(8,128)(2,1)S(1)}) custom-call(bf16[16,2304]{1,0:T(8,128)(2,1)S(1)} %bitcast.12, bf16[16,2304]{1,0:T(8,128)(2,1)S(1)} %collective-permute-done.refs_1_, bf16[2304,512]{1,0:T(8,128)(2,1)S(1)} %shard_map.55.refs_2_, bf16[2304,512]{1,0:T(8,128)(2,1)S(1)} %collective-permute-done.1.refs_3_), custom_call_target="tpu_custom_call" | custom-call | tf_op jit(solution)/shard_map/pallas_call | solution.py:66
  13.2 1.5 %collective-permute-start.2 = (bf16[64,512]{1,0:T(8,128)(2,1)S(1)}, bf16[64,512]{1,0:T(8,128)(2,1)S(1)}, u32[]{:S(2)}, u32[]{:S(2)}) collective-permute-start(bf16[64,512]{1,0:T(8,128)(2,1)S(1)} %get-tuple-element.14), channel_id=1, source_target_pairs={{0,8},{8,0},{16,24},{24,16},{1,9},{9,1},{17,25},{25,17},{2,10},{10... | collective-permute-start | bytes 196616 | tf_op jit(solution)/shard_map/ppermute | solution.py:137
  14.7 0.0 collective-permute-done.9
  14.7 1.1 %collective-permute-start.10 = (bf16[64,512]{1,0:T(8,128)(2,1)S(1)}, bf16[64,512]{1,0:T(8,128)(2,1)S(1)}, u32[]{:S(2)}, u32[]{:S(2)}) collective-permute-start(bf16[64,512]{1,0:T(8,128)(2,1)S(1)} %get-tuple-element.21), channel_id=1, source_target_pairs={{0,8},{8,0},{16,24},{24,16},{1,9},{9,1},{17,25},{25,17},{2,10},{10... | collective-permute-start | bytes 196616 | tf_op jit(solution)/shard_map/ppermute | solution.py:137
  15.8 1.9 %collective-permute-done.2 = bf16[64,512]{1,0:T(8,128)(2,1)S(1)} collective-permute-done((bf16[64,512]{1,0:T(8,128)(2,1)S(1)}, bf16[64,512]{1,0:T(8,128)(2,1)S(1)}, u32[]{:S(2)}, u32[]{:S(2)}) %collective-permute-start.2) | collective-permute-done | bytes 65568 | tf_op jit(solution)/shard_map/ppermute | solution.py:137
  17.8 1.4 %collective-permute-start.3 = (bf16[64,512]{1,0:T(8,128)(2,1)S(1)}, bf16[64,512]{1,0:T(8,128)(2,1)S(1)}, u32[]{:S(2)}, u32[]{:S(2)}) collective-permute-start(bf16[64,512]{1,0:T(8,128)(2,1)S(1)} %get-tuple-element.23), channel_id=1, source_target_pairs={{0,16},{8,24},{16,0},{24,8},{1,17},{9,25},{17,1},{25,9},{2,18},{10... | collective-permute-start | bytes 196616 | tf_op jit(solution)/shard_map/ppermute | solution.py:137
  19.1 0.0 copy-done.3
  19.2 0.0 collective-permute-start.4
  19.2 1.2 %collective-permute-done.4 = f32[512]{0:T(512)S(1)} collective-permute-done((f32[512]{0:T(512)S(1)}, f32[512]{0:T(512)S(1)}, u32[]{:S(2)}, u32[]{:S(2)}) %collective-permute-start.4) | collective-permute-done | bytes 2080 | tf_op jit(solution)/shard_map/ppermute | solution.py:137
  20.3 0.0 collective-permute-done.5.far_ref
  20.3 0.0 collective-permute-done.10.other_ref
  20.3 0.0 copy-done
  20.3 0.9 %shard_map.59 = (bf16[16,2304]{1,0:T(8,128)(2,1)S(1)}, bf16[16,2304]{1,0:T(8,128)(2,1)S(1)}) custom-call(f32[64,512]{1,0:T(8,128)S(1)} %get-tuple-element.22.share_ref, bf16[64,512]{1,0:T(8,128)(2,1)S(1)} %collective-permute-done.10.other_ref, f32[1,512]{1,0:T(1,128)S(1)} %bitcast.13, f32[1,512]{1,0:T(1,128)S(1)} %bitcast.15, bf16[512,2304]{1,0:T(8,128)(2,1)S(1)} %bitcast.7, ...), custom_call_target="tpu_custom_call" | custom-call | tf_op jit(solution)/shard_map/pallas_call | solution.py:87
  21.2 2.2 %collective-permute-start.11 = (bf16[16,2304]{1,0:T(8,128)(2,1)S(1)}, bf16[16,2304]{1,0:T(8,128)(2,1)S(1)}, u32[]{:S(2)}, u32[]{:S(2)}) collective-permute-start(bf16[16,2304]{1,0:T(8,128)(2,1)S(1)} %get-tuple-element.19), channel_id=1, source_target_pairs={{5,0},{4,1},{7,2},{6,3},{1,4},{0,5},{3,6},{2,7},{13,8},{12,9},{15,... | collective-permute-start | bytes 221192 | tf_op jit(solution)/shard_map/ppermute | solution.py:137
  23.5 0.8 %collective-permute-start.12 = (bf16[16,2304]{1,0:T(8,128)(2,1)S(1)}, bf16[16,2304]{1,0:T(8,128)(2,1)S(1)}, u32[]{:S(2)}, u32[]{:S(2)}) collective-permute-start(bf16[16,2304]{1,0:T(8,128)(2,1)S(1)} %get-tuple-element.20), channel_id=1, source_target_pairs={{3,0},{2,1},{1,2},{0,3},{7,4},{6,5},{5,6},{4,7},{11,8},{10,9},{9,1... | collective-permute-start | bytes 221192 | tf_op jit(solution)/shard_map/ppermute | solution.py:137
  24.2 0.0 collective-permute-done.3.other_ref
  24.2 0.0 copy-start.2
  24.2 0.9 %shard_map.57 = (f32[16,2304]{1,0:T(8,128)S(1)}, bf16[16,2304]{1,0:T(8,128)(2,1)S(1)}) custom-call(f32[64,512]{1,0:T(8,128)S(1)} %get-tuple-element.24.share_ref, bf16[64,512]{1,0:T(8,128)(2,1)S(1)} %collective-permute-done.3.other_ref, f32[1,512]{1,0:T(1,128)S(1)} %bitcast.14, f32[1,512]{1,0:T(1,128)S(1)} %bitcast.16, bf16[512,2304]{1,0:T(8,128)(2,1)S(1)} %bitcast.8, ...), custom_call_target="tpu_custom_call" | custom-call | tf_op jit(solution)/shard_map/pallas_call | solution.py:87
  25.1 1.1 %collective-permute-start.6 = (bf16[16,2304]{1,0:T(8,128)(2,1)S(1)}, bf16[16,2304]{1,0:T(8,128)(2,1)S(1)}, u32[]{:S(2)}, u32[]{:S(2)}) collective-permute-start(bf16[16,2304]{1,0:T(8,128)(2,1)S(1)} %get-tuple-element.16), channel_id=1, source_target_pairs={{7,0},{6,1},{5,2},{4,3},{3,4},{2,5},{1,6},{0,7},{15,8},{14,9},{13,... | collective-permute-start | bytes 221192 | tf_op jit(solution)/shard_map/ppermute | solution.py:137
  26.3 0.1 collective-permute-done.11.refs_1_
  26.4 1.5 %collective-permute-done.12.refs_2_ = bf16[16,2304]{1,0:T(8,128)(2,1)S(1)} collective-permute-done((bf16[16,2304]{1,0:T(8,128)(2,1)S(1)}, bf16[16,2304]{1,0:T(8,128)(2,1)S(1)}, u32[]{:S(2)}, u32[]{:S(2)}) %collective-permute-start.12) | collective-permute-done | bytes 73760 | tf_op jit(solution)/shard_map/ppermute | solution.py:137
  27.9 3.2 %collective-permute-done.6.refs_0_ = bf16[16,2304]{1,0:T(8,128)(2,1)S(1)} collective-permute-done((bf16[16,2304]{1,0:T(8,128)(2,1)S(1)}, bf16[16,2304]{1,0:T(8,128)(2,1)S(1)}, u32[]{:S(2)}, u32[]{:S(2)}) %collective-permute-start.6) | collective-permute-done | bytes 73760 | tf_op jit(solution)/shard_map/ppermute | solution.py:137
  31.1 0.0 copy-done.2
  31.1 0.7 %shard_map.60 = bf16[16,2304]{1,0:T(8,128)(2,1)} custom-call(f32[16,2304]{1,0:T(8,128)S(1)} %get-tuple-element.15.own_ref, f32[1,2304]{1,0:T(1,128)S(1)} %copy-done.2, bf16[16,2304]{1,0:T(8,128)(2,1)S(1)} %collective-permute-done.6.refs_0_, bf16[16,2304]{1,0:T(8,128)(2,1)S(1)} %collective-permute-done.11.refs_1_, ...), custom_call_target="tpu_custom_call" | custom-call | tf_op jit(solution)/shard_map/pallas_call | solution.py:115
  (2 shorter events, 0.0 us)
Async XLA Ops:
  0.0 8.9 %collective-permute-start.1 = (bf16[2304,512]{1,0:T(8,128)(2,1)}, bf16[2304,512]{1,0:T(8,128)(2,1)S(1)}, u32[]{:S(2)}, u32[]{:S(2)}) collective-permute-start(bf16[2304,512]{1,0:T(8,128)(2,1)} %bitcast.17), channel_id=1, source_target_pairs={{0,1},{1,0},{2,3},{3,2},{4,5},{5,4},{6,7},{7,6},{8,9},{9,8},{10,11... | collective-permute-start | bytes 7077896 | tf_op jit(solution)/shard_map/ppermute | solution.py:137
  0.5 19.8 %collective-permute-start.5 = (bf16[512,2304]{1,0:T(8,128)(2,1)}, bf16[512,2304]{1,0:T(8,128)(2,1)S(1)}, u32[]{:S(2)}, u32[]{:S(2)}) collective-permute-start(bf16[512,2304]{1,0:T(8,128)(2,1)} %bitcast.6), channel_id=1, source_target_pairs={{0,1},{1,0},{2,3},{3,2},{4,5},{5,4},{6,7},{7,6},{8,9},{9,8},{10,11... | collective-permute-start | bytes 7077896 | tf_op jit(solution)/shard_map/ppermute | solution.py:137
  0.5 7.0 %collective-permute-start.8 = (bf16[16,2304]{1,0:T(8,128)(2,1)}, bf16[16,2304]{1,0:T(8,128)(2,1)S(1)}, u32[]{:S(2)}, u32[]{:S(2)}) collective-permute-start(bf16[16,2304]{1,0:T(8,128)(2,1)} %bitcast.9), channel_id=1, source_target_pairs={{0,3},{1,2},{2,1},{3,0},{4,7},{5,6},{6,5},{7,4},{8,11},{9,10},{10,... | collective-permute-start | bytes 221192 | tf_op jit(solution)/shard_map/ppermute | solution.py:137
  3.2 5.7 %collective-permute-start.7 = (bf16[16,2304]{1,0:T(8,128)(2,1)}, bf16[16,2304]{1,0:T(8,128)(2,1)S(1)}, u32[]{:S(2)}, u32[]{:S(2)}) collective-permute-start(bf16[16,2304]{1,0:T(8,128)(2,1)} %bitcast.10), channel_id=1, source_target_pairs={{0,5},{1,4},{2,7},{3,6},{4,1},{5,0},{6,3},{7,2},{8,13},{9,12},{10,... | collective-permute-start | bytes 221192 | tf_op jit(solution)/shard_map/ppermute | solution.py:137
  5.9 6.4 %collective-permute-start = (bf16[16,2304]{1,0:T(8,128)(2,1)}, bf16[16,2304]{1,0:T(8,128)(2,1)S(1)}, u32[]{:S(2)}, u32[]{:S(2)}) collective-permute-start(bf16[16,2304]{1,0:T(8,128)(2,1)} %bitcast.11), channel_id=1, source_target_pairs={{0,7},{1,6},{2,5},{3,4},{4,3},{5,2},{6,1},{7,0},{8,15},{9,14},{10,... | collective-permute-start | bytes 221192 | tf_op jit(solution)/shard_map/ppermute | solution.py:137
  7.5 4.8 %copy-start.1 = (bf16[16,1,2304]{2,0,1:T(8,128)(2,1)S(1)}, bf16[16,1,2304]{2,0,1:T(8,128)(2,1)}, u32[]{:S(2)}) copy-start(bf16[16,1,2304]{2,0,1:T(8,128)(2,1)} %param.5) | copy-start | bytes 221188
  9.8 9.4 %copy-start.3 = (f32[512]{0:T(512)S(1)}, f32[512]{0:T(512)}, u32[]{:S(2)}) copy-start(f32[512]{0:T(512)} %param.7) | copy-start | bytes 6148
  9.8 10.5 %copy-start = (bf16[1,512,2304]{2,1,0:T(8,128)(2,1)S(1)}, bf16[1,512,2304]{2,1,0:T(8,128)(2,1)}, u32[]{:S(2)}) copy-start(bf16[1,512,2304]{2,1,0:T(8,128)(2,1)} %param.8) | copy-start | bytes 7077892
  9.8 4.9 %collective-permute-start.9 = (bf16[64,512]{1,0:T(8,128)(2,1)S(1)}, bf16[64,512]{1,0:T(8,128)(2,1)S(1)}, u32[]{:S(2)}, u32[]{:S(2)}) collective-permute-start(bf16[64,512]{1,0:T(8,128)(2,1)S(1)} %get-tuple-element.18), channel_id=1, source_target_pairs={{0,16},{8,24},{16,0},{24,8},{1,17},{9,25},{17,1},{25,9},{2,18},{10... | collective-permute-start | bytes 196616 | tf_op jit(solution)/shard_map/ppermute | solution.py:137
  13.2 4.6 %collective-permute-start.2 = (bf16[64,512]{1,0:T(8,128)(2,1)S(1)}, bf16[64,512]{1,0:T(8,128)(2,1)S(1)}, u32[]{:S(2)}, u32[]{:S(2)}) collective-permute-start(bf16[64,512]{1,0:T(8,128)(2,1)S(1)} %get-tuple-element.14), channel_id=1, source_target_pairs={{0,8},{8,0},{16,24},{24,16},{1,9},{9,1},{17,25},{25,17},{2,10},{10... | collective-permute-start | bytes 196616 | tf_op jit(solution)/shard_map/ppermute | solution.py:137
  14.7 5.6 %collective-permute-start.10 = (bf16[64,512]{1,0:T(8,128)(2,1)S(1)}, bf16[64,512]{1,0:T(8,128)(2,1)S(1)}, u32[]{:S(2)}, u32[]{:S(2)}) collective-permute-start(bf16[64,512]{1,0:T(8,128)(2,1)S(1)} %get-tuple-element.21), channel_id=1, source_target_pairs={{0,8},{8,0},{16,24},{24,16},{1,9},{9,1},{17,25},{25,17},{2,10},{10... | collective-permute-start | bytes 196616 | tf_op jit(solution)/shard_map/ppermute | solution.py:137
  17.8 6.5 %collective-permute-start.3 = (bf16[64,512]{1,0:T(8,128)(2,1)S(1)}, bf16[64,512]{1,0:T(8,128)(2,1)S(1)}, u32[]{:S(2)}, u32[]{:S(2)}) collective-permute-start(bf16[64,512]{1,0:T(8,128)(2,1)S(1)} %get-tuple-element.23), channel_id=1, source_target_pairs={{0,16},{8,24},{16,0},{24,8},{1,17},{9,25},{17,1},{25,9},{2,18},{10... | collective-permute-start | bytes 196616 | tf_op jit(solution)/shard_map/ppermute | solution.py:137
  19.2 1.2 %collective-permute-start.4 = (f32[512]{0:T(512)S(1)}, f32[512]{0:T(512)S(1)}, u32[]{:S(2)}, u32[]{:S(2)}) collective-permute-start(f32[512]{0:T(512)S(1)} %copy-done.3), channel_id=1, source_target_pairs={{0,1},{1,0},{2,3},{3,2},{4,5},{5,4},{6,7},{7,6},{8,9},{9,8},{10,11... | collective-permute-start | bytes 6152 | tf_op jit(solution)/shard_map/ppermute | solution.py:137
  21.2 5.1 %collective-permute-start.11 = (bf16[16,2304]{1,0:T(8,128)(2,1)S(1)}, bf16[16,2304]{1,0:T(8,128)(2,1)S(1)}, u32[]{:S(2)}, u32[]{:S(2)}) collective-permute-start(bf16[16,2304]{1,0:T(8,128)(2,1)S(1)} %get-tuple-element.19), channel_id=1, source_target_pairs={{5,0},{4,1},{7,2},{6,3},{1,4},{0,5},{3,6},{2,7},{13,8},{12,9},{15,... | collective-permute-start | bytes 221192 | tf_op jit(solution)/shard_map/ppermute | solution.py:137
  23.5 4.4 %collective-permute-start.12 = (bf16[16,2304]{1,0:T(8,128)(2,1)S(1)}, bf16[16,2304]{1,0:T(8,128)(2,1)S(1)}, u32[]{:S(2)}, u32[]{:S(2)}) collective-permute-start(bf16[16,2304]{1,0:T(8,128)(2,1)S(1)} %get-tuple-element.20), channel_id=1, source_target_pairs={{3,0},{2,1},{1,2},{0,3},{7,4},{6,5},{5,6},{4,7},{11,8},{10,9},{9,1... | collective-permute-start | bytes 221192 | tf_op jit(solution)/shard_map/ppermute | solution.py:137
  24.2 6.9 %copy-start.2 = (f32[1,2304]{1,0:T(1,128)S(1)}, f32[1,2304]{1,0:T(1,128)}, u32[]{:S(2)}) copy-start(f32[1,2304]{1,0:T(1,128)} %bias_ref.1) | copy-start | bytes 27652
  25.1 6.0 %collective-permute-start.6 = (bf16[16,2304]{1,0:T(8,128)(2,1)S(1)}, bf16[16,2304]{1,0:T(8,128)(2,1)S(1)}, u32[]{:S(2)}, u32[]{:S(2)}) collective-permute-start(bf16[16,2304]{1,0:T(8,128)(2,1)S(1)} %get-tuple-element.16), channel_id=1, source_target_pairs={{7,0},{6,1},{5,2},{4,3},{3,4},{2,5},{1,6},{0,7},{15,8},{14,9},{13,... | collective-permute-start | bytes 221192 | tf_op jit(solution)/shard_map/ppermute | solution.py:137
